TPU v7x, 32 devices: a whole 2x2x4 slice. The times are simulated.
32 devices in a mesh: ang: 16 (over z, x, core), strip: 2 (over y).
Axes of the slice: x: 2, y: 2, z: 4, core: 2. Of those that a mesh axis runs over, the one named last changes fastest.
Arguments:
- measured: float32 [16, 16, 128, 128], P('ang', 'strip'), may hold values from 0.05 to 4
- positions: int32 [16, 16], P('ang', 'strip'), may hold values from 0 to 384
- probe_field: float32 [2, 128, 128], replicated, may hold values from -6 to 6
- object_field: float32 [16, 512, 2, 128], P('ang', 'strip'), may hold values from -6 to 6
- dual_field: float32 [16, 512, 2, 128], P('ang', 'strip'), may hold values from -6 to 6
- volume: float32 [8192, 2, 128], P(('ang', 'strip')), may hold values from -6 to 6
- radon_tiles: bfloat16 [32, 16, 2, 32, 256], P(('ang', 'strip')), may hold values from -0.1875 to 0.1875
- tile_range: int32 [16, 16, 2, 1], P('ang', None, 'strip'), may hold values from 0 to 14
Outputs:
- object_next: float32 [16, 512, 2, 128], P('ang', 'strip')
- dual_next: float32 [16, 512, 2, 128], P('ang', 'strip')
- volume_next: float32 [8192, 2, 128], P(('ang', 'strip'))
Inputs may be any that keep to these rules, and one draw needn't show every extreme that they name: `positions`: a frame covers 128 detector columns from its position. A pixel tile meets ray tiles tile_range to tile_range + 1 at that angle.
All inputs are finite; a program needn't handle non-finite values.
Results may differ from a plain program's by a relative error of at most 0.0027.
Values may be sent and summed in bfloat16 or wider, within the bound.
A program may use at most 64 MiB of HBM per device.

v0:
```python
import functools
import math

import jax
import jax.numpy as jnp
import numpy as np
from jax import lax
from jax.experimental import pallas as pl
from jax.experimental.pallas import tpu as pltpu
from jax.sharding import PartitionSpec as P

RAYS = 32
VMEM_BYTES = 67043328

penalty = 1.0
object_step = 0.1
volume_step = 1.0
MESH = pl.DeviceIdType.MESH


def dft_tables(length):
    indices = np.arange(length, dtype=np.int64)
    angles = (indices[:, None] * indices[None, :] % length) * (2.0 * math.pi / length)
    scaling = 1.0 / math.sqrt(length)
    parts = []
    for table in (np.cos(angles) * scaling, np.sin(angles) * scaling):
        table = table.astype(np.float32)
        high = table.astype(jnp.bfloat16)
        parts += [high, (table - high.astype(np.float32)).astype(jnp.bfloat16)]
    return np.stack(parts)


def split(value):
    high = value.astype(jnp.bfloat16)
    return high, (value - high.astype(jnp.float32)).astype(jnp.bfloat16)


def dot(left, right):
    return jnp.dot(left, right, preferred_element_type=jnp.float32)


def dot3(left, right):
    return dot(left[0], right[0]) + (dot(left[0], right[1]) + dot(left[1], right[0]))


def beside(left, right):
    return jnp.concatenate([left, right], axis=1)


def above(top, low):
    return jnp.concatenate([top, low], axis=0)


def swap_blocks(value):
    half = value.shape[1] // 2
    return above(
        beside(value[:half, :half], value[half:, :half]),
        beside(value[:half, half:], value[half:, half:]),
    )


def both_parts(ref, columns):
    return beside(ref[pl.ds(0, columns, stride=2), :], ref[pl.ds(1, columns, stride=2), :])


def put_parts(ref, value):
    columns, half = value.shape[0], value.shape[1] // 2
    ref[pl.ds(0, columns, stride=2), :] = value[:, :half]
    ref[pl.ds(1, columns, stride=2), :] = value[:, half:]


def window(start, count, rows):
    first = lax.broadcasted_iota(jnp.int32, (count, rows), 0) + start
    return one_where(first == lax.broadcasted_iota(jnp.int32, (count, rows), 1))


def one_where(mask):
    return jnp.where(mask, 1.0, 0.0).astype(jnp.bfloat16)


def one_hot(rows, starts, count, width, scale):
    lanes = lax.broadcasted_iota(jnp.int32, (1, count * width), 1)
    block = lanes // width
    target = lanes % width
    for k in range(count):
        target = target + jnp.where(block == k, starts[k] * scale, 0)
    row = lax.broadcasted_iota(jnp.int32, (rows, count * width), 0)
    return one_where(row == target)


def xor(left, right, bound):
    result, bit = 0, 1
    while bit < bound:
        result = result + ((left // bit) + (right // bit)) % 2 * bit
        bit *= 2
    return result


def kernel(
    angles, strips,
    positions, ranges, measured_hbm, probe_hbm, field_hbm, dual_hbm, volume_hbm, radon_hbm,
    tables_hbm,
    object_next, dual_next, volume_next,
    measured, probe, field, dual, volume, radon, tables,
    ray_out, ray_in, pick_out, pick_in, field_out, field_in, grad_out, grad_in,
    dense_out, dense_in, rows_half, whole_field, grads, total_grad, total_rays, turned_radon,
    picker, selector,
    load_sem, ray_send, ray_recv, pick_send, pick_recv, strip_send, strip_recv,
):
    loads = {}
    for k, (name, source, target) in enumerate((
        ("volume", volume_hbm, volume), ("radon", radon_hbm, radon), ("field", field_hbm, field),
        ("tables", tables_hbm, tables), ("probe", probe_hbm, probe),
        ("measured", measured_hbm, measured), ("dual", dual_hbm, dual),
    )):
        loads[name] = pltpu.make_async_copy(source, target, load_sem.at[k])
        loads[name].start()
    me, strip = lax.axis_index("ang"), lax.axis_index("strip")
    columns = field.shape[0] // 2
    detector = strips * columns
    frames, side = measured.shape[0], measured.shape[1]
    slices = field.shape[1]
    chunks, hit_rows = ray_out.shape[0], ray_out.shape[2]
    if angles & (angles - 1):
        ang_peers = [lax.rem(me + offset, angles) for offset in range(1, angles)]
    else:
        ang_peers = [xor(me, offset, angles) for offset in range(angles - 1, 0, -1)]
    strip_peers = [lax.rem(strip + offset, strips) for offset in range(1, strips)]

    def rows_of(owner):
        return pl.ds(pl.multiple_of(owner * columns, columns), columns)

    barrier = pltpu.get_barrier_semaphore()
    for peer in ang_peers:
        pl.semaphore_signal(barrier, inc=1, device_id=(peer, strip), device_id_type=MESH)
    for peer in strip_peers:
        pl.semaphore_signal(barrier, inc=1, device_id=(me, peer), device_id_type=MESH)

    loads["volume"].wait()
    loads["radon"].wait()
    pixels = volume.shape[0] // 2
    volume_half = both_parts(volume, pixels).astype(jnp.bfloat16)
    sums = dot(radon[...], volume_half).astype(jnp.bfloat16)
    for c in range(chunks):
        ray_out[c] = sums[:, c * slices:(c + 1) * slices].reshape(ray_out.shape[1:])
    loads["field"].wait()
    own_field = both_parts(field, columns)
    field_out[...] = own_field.astype(jnp.bfloat16)
    pl.semaphore_wait(barrier, len(ang_peers) + len(strip_peers))

    def strip_copy(source, target, stage, slot, peer):
        return pltpu.make_async_remote_copy(
            src_ref=source, dst_ref=target,
            send_sem=strip_send.at[stage, peer], recv_sem=strip_recv.at[stage, slot],
            device_id=(me, peer), device_id_type=MESH,
        )

    def ray_copy(c, slot, peer):
        return pltpu.make_async_remote_copy(
            src_ref=ray_out.at[c, peer], dst_ref=ray_in.at[c, slot],
            send_sem=ray_send.at[c, peer], recv_sem=ray_recv.at[c, slot],
            device_id=(peer, strip), device_id_type=MESH,
        )

    def pick_copy(c, slot, peer):
        return pltpu.make_async_remote_copy(
            src_ref=pick_out.at[c, peer], dst_ref=pick_in.at[c, slot],
            send_sem=pick_send.at[c, peer], recv_sem=pick_recv.at[c, slot],
            device_id=(peer, strip), device_id_type=MESH,
        )

    def grad_copy(c, slot, peer):
        return strip_copy(grad_out.at[c, peer], grad_in.at[c, slot], 1 + c, slot, peer)

    def dense_copy(c, slot, peer):
        return strip_copy(
            dense_out.at[c, peer], dense_in.at[c, slot], 1 + chunks + c, slot, peer
        )

    def residual_copy(c, owner, peer):
        part = rows_half.at[c, rows_of(owner), :]
        return strip_copy(part, part, 1 + 2 * chunks + c, owner, peer)

    started = []

    def start(copy):
        copy.start()
        started.append(copy)

    for peer in ang_peers:
        start(ray_copy(0, me, peer))
    for peer in strip_peers:
        start(strip_copy(field_out, field_in.at[strip], 0, strip, peer))
    for c in range(1, chunks):
        for peer in ang_peers:
            start(ray_copy(c, me, peer))

    for c in range(chunks):
        ray_in[c, me] = ray_out[c, me]
    selector[...] = one_hot(
        detector, [ranges[k] for k in range(angles)], angles, hit_rows, RAYS
    )
    for name in ("tables", "probe", "measured", "dual"):
        loads[name].wait()
    cos_high, cos_low, sin_high, sin_low = (tables[k] for k in range(4))
    turn = tuple(
        above(beside(c, -s), beside(s, c)) for c, s in ((cos_high, sin_high), (cos_low, sin_low))
    )
    back_turn = tuple(
        above(beside(c, s), beside(-s, c)) for c, s in ((cos_high, sin_high), (cos_low, sin_low))
    )
    probe_re, probe_im = probe[0], probe[1]
    whole_field[rows_of(strip), :] = own_field
    for peer in strip_peers:
        strip_copy(field_out, field_in.at[peer], 0, peer, peer).wait_recv()
        whole_field[rows_of(peer), :] = field_in[peer].astype(jnp.float32)
    field_high, field_low = split(whole_field[...])

    def frame_pair(pair):
        waves = []
        for j in (pair, pair + 1):
            cut = window(positions[j], side, detector)
            patch = dot(cut, field_high) + dot(cut, field_low)
            re, im = patch[:, :side], patch[:, side:]
            waves.append(beside(probe_re * re - probe_im * im, probe_re * im + probe_im * re))
        right = dot3(split(above(*waves)), turn)
        far = dot3(back_turn, split(swap_blocks(right)))
        far_re, far_im = far[:side], far[side:]
        modulus = jnp.sqrt(far_re * far_re + far_im * far_im)
        intensity = beside(measured[pair], measured[pair + 1])
        shrink = 1.0 - jnp.sqrt(intensity) / jnp.maximum(modulus, 1.0)
        left = dot3(turn, split(above(far_re * shrink, far_im * shrink)))
        back = dot3(split(swap_blocks(left)), back_turn)
        for k in range(2):
            part = back[k * side:(k + 1) * side]
            re, im = part[:, :side], part[:, side:]
            grads[(pair + k) * side:(pair + k + 1) * side, :] = beside(
                probe_re * re + probe_im * im, probe_re * im - probe_im * re
            )

    def sum_rays(c):
        for peer in ang_peers:
            ray_copy(c, peer, peer).wait_recv()
        total_rays[c] = dot(selector[...], ray_in[c].reshape(angles * hit_rows, slices))
        for k in range(strips):
            dense_out[c, k] = total_rays[c, k * columns:(k + 1) * columns].astype(jnp.bfloat16)
        for peer in strip_peers:
            start(dense_copy(c, strip, peer))

    middle = frames // 4 * 2
    for pair in range(0, middle, 2):
        frame_pair(pair)
    sum_rays(0)
    for pair in range(middle, frames, 2):
        frame_pair(pair)
    deposit = one_hot(detector, [positions[j] for j in range(frames)], frames, side, 1)
    high, low = split(grads[...])
    deposited = dot(deposit, high) + dot(deposit, low)
    for c in range(chunks):
        total_grad[c] = deposited[:, c * slices:(c + 1) * slices]
        for k in range(strips):
            grad_out[c, k] = total_grad[c, k * columns:(k + 1) * columns].astype(jnp.bfloat16)
        for peer in strip_peers:
            start(grad_copy(c, strip, peer))
    for c in range(1, chunks):
        sum_rays(c)
    for k in range(angles):
        picker[k] = window(ranges[k] * RAYS, hit_rows, detector)

    for c in range(chunks):
        intersection = total_grad[c, rows_of(strip), :]
        for peer in strip_peers:
            grad_copy(c, peer, peer).wait_recv()
            intersection = intersection + grad_in[c, peer].astype(jnp.float32)
        projection = total_rays[c, rows_of(strip), :]
        for peer in strip_peers:
            dense_copy(c, peer, peer).wait_recv()
            projection = projection + dense_in[c, peer].astype(jnp.float32)
        part = pl.ds(c, columns, stride=chunks)
        part_field, part_dual = field[part, :], dual[part, :]
        updated = part_field - object_step * (
            intersection + part_dual + penalty * (part_field - projection)
        )
        residual = penalty * (projection - updated) - part_dual
        rows_half[c, rows_of(strip), :] = residual.astype(jnp.bfloat16)
        for peer in strip_peers:
            start(residual_copy(c, strip, peer))
        object_next[part, :] = updated
        dual_next[part, :] = part_dual + penalty * (updated - projection)
    for c in range(chunks):
        for peer in strip_peers:
            residual_copy(c, peer, peer).wait_recv()
        rows = rows_half[c]
        for peer in ang_peers:
            pick_out[c, peer] = dot(picker[peer], rows).astype(jnp.bfloat16)
            start(pick_copy(c, me, peer))
        pick_in[c, me] = dot(picker[me], rows).astype(jnp.bfloat16)
    turned_radon[...] = radon[...].T
    for c in range(chunks):
        for peer in ang_peers:
            pick_copy(c, peer, peer).wait_recv()
        gradient = dot(turned_radon[...], pick_in[c].reshape(angles * hit_rows, slices))
        part = pl.ds(c, pixels, stride=chunks)
        volume_next[part, :] = volume[part, :] - volume_step * gradient
    for copy in started:
        copy.wait_send()


def body(
    measured, positions, probe_field, object_field, dual_field, volume, radon_tiles, tile_range
):
    angles, strips = lax.axis_size("ang"), lax.axis_size("strip")
    frames, side = measured.shape[1], measured.shape[2]
    columns, width = object_field.shape[1], object_field.shape[2] * object_field.shape[3]
    hit_rows = radon_tiles.shape[2] * radon_tiles.shape[3]
    pixels = radon_tiles.shape[4]
    chunks, slices = object_field.shape[2], object_field.shape[3]
    vmem = pl.BlockSpec(memory_space=pltpu.VMEM)
    smem = pl.BlockSpec(memory_space=pltpu.SMEM)
    half = jnp.bfloat16
    outs = pl.pallas_call(
        functools.partial(kernel, angles, strips),
        out_shape=(
            jax.ShapeDtypeStruct((2 * columns, slices), jnp.float32),
            jax.ShapeDtypeStruct((2 * columns, slices), jnp.float32),
            jax.ShapeDtypeStruct((2 * pixels, slices), jnp.float32),
        ),
        in_specs=[smem, smem] + [pl.BlockSpec(memory_space=pltpu.HBM)] * 7,
        out_specs=(vmem, vmem, vmem),
        scratch_shapes=[
            pltpu.VMEM((frames, side, side), jnp.float32),
            pltpu.VMEM((chunks, side, side), jnp.float32),
            pltpu.VMEM((chunks * columns, slices), jnp.float32),
            pltpu.VMEM((chunks * columns, slices), jnp.float32),
            pltpu.VMEM((chunks * pixels, slices), jnp.float32),
            pltpu.VMEM((angles * hit_rows, pixels), half),
            pltpu.VMEM((4, side, side), half),
        ] + [pltpu.VMEM((chunks, angles, hit_rows, slices), half)] * 4 + [
            pltpu.VMEM((columns, width), half),
            pltpu.VMEM((strips, columns, width), half),
        ] + [pltpu.VMEM((chunks, strips, columns, slices), half)] * 4 + [
            pltpu.VMEM((chunks, strips * columns, slices), half),
            pltpu.VMEM((strips * columns, width), jnp.float32),
            pltpu.VMEM((frames * side, width), jnp.float32),
            pltpu.VMEM((chunks, strips * columns, slices), jnp.float32),
            pltpu.VMEM((chunks, strips * columns, slices), jnp.float32),
            pltpu.VMEM((pixels, angles * hit_rows), half),
            pltpu.VMEM((angles, hit_rows, strips * columns), half),
            pltpu.VMEM((strips * columns, angles * hit_rows), half),
            pltpu.SemaphoreType.DMA((7,)),
        ] + [pltpu.SemaphoreType.DMA((chunks, angles))] * 4
        + [pltpu.SemaphoreType.DMA((1 + 3 * chunks, strips))] * 2,
        compiler_params=pltpu.CompilerParams(
            collective_id=0, has_side_effects=True, vmem_limit_bytes=VMEM_BYTES
        ),
    )(
        positions.reshape(frames),
        tile_range.reshape(angles),
        measured[0],
        probe_field,
        object_field.reshape(2 * columns, slices),
        dual_field.reshape(2 * columns, slices),
        volume.reshape(2 * pixels, slices),
        radon_tiles.reshape(angles * hit_rows, pixels),
        jnp.asarray(dft_tables(side)),
    )
    return (
        outs[0].reshape(object_field.shape),
        outs[1].reshape(dual_field.shape),
        outs[2].reshape(volume.shape),
    )


def solution(mesh):
    return jax.shard_map(
        body,
        mesh=mesh,
        in_specs=(
            P("ang", "strip", None, None),
            P("ang", "strip"),
            P(),
            P("ang", "strip", None, None),
            P("ang", "strip", None, None),
            P(("ang", "strip"), None, None),
            P(("ang", "strip"), None, None, None, None),
            P("ang", None, "strip", None),
        ),
        out_specs=(
            P("ang", "strip", None, None),
            P("ang", "strip", None, None),
            P(("ang", "strip"), None, None),
        ),
        check_vma=False,
    )
```

profile of v0, /device:TPU:0, one launch (start us, length us, event | category | flops | bytes accessed | tf_op | source)
XLA Modules:
  0.0 45.9 jit_solution(15059019979179958499)
XLA Ops:
  0.6 41.8 %shard_map.112 = (f32[512,128]{1,0:T(8,128)}, f32[512,128]{1,0:T(8,128)}, f32[512,128]{1,0:T(8,128)}) custom-call(s32[8]{0:T(128)} %bitcast.18, s32[16]{0:T(128)} %bitcast.19, f32[8,128,128]{2,1,0:T(8,128)} %bitcast.10, f32[2,128,128]{2,1,0:T(8,128)} %probe_hbm.1, f32[512,128]{1,0:T(8,128)} %bitcast.15, f32[512,128]{1,0:T(8,128)} %bitcast.16, ...), custom_call_target="tpu_custom_call" | custom-call | tf_op jit(solution)/shard_map/pallas_call | solution.py:321
  42.4 0.0 copy-start.1
  42.4 1.7 %copy.15 = f32[1,256,2,128]{3,2,1,0:T(2,128)} copy(f32[1,256,2,128]{3,2,1,0:T(2,128)} %bitcast.14) | data formatting | bytes 524288
  44.2 0.0 copy-done.1
  44.2 0.0 copy-start
  44.2 0.7 %copy.16 = f32[1,256,2,128]{3,2,1,0:T(2,128)} copy(f32[1,256,2,128]{3,2,1,0:T(2,128)S(1)} %bitcast.13) | data formatting | bytes 524288
  44.9 0.3 copy-done
  45.2 0.7 %copy.17 = f32[256,2,128]{2,1,0:T(2,128)} copy(f32[256,2,128]{2,1,0:T(2,128)S(1)} %bitcast.12) | data formatting | bytes 524288
Async XLA Ops:
  42.4 1.7 %copy-start.1 = (f32[512,128]{1,0:T(8,128)S(1)}, f32[512,128]{1,0:T(8,128)}, u32[]{:S(2)}) copy-start(f32[512,128]{1,0:T(8,128)} %get-tuple-element.7) | copy-start | bytes 786436
  44.2 1.0 %copy-start = (f32[512,128]{1,0:T(8,128)S(1)}, f32[512,128]{1,0:T(8,128)}, u32[]{:S(2)}) copy-start(f32[512,128]{1,0:T(8,128)} %get-tuple-element.8) | copy-start | bytes 786436
where the time goes:
time: 46.1 us; the launch traced here: 45.9 us
  Pallas kernels  41.8 us (91%)
  local copies, waits for them, and re-layouts  3.46 us (8%)
  between operations  0.65 us (1%)
    pallas_call x1, Pallas kernels, body(): pl.pallas_call(functools.partial(kernel, angles, strips), out_shape=(jax....  41.8 us
    unnamed x7, local copies, waits for them, and re-layouts  3.46 us

commit v1 on v0

--- a/solution.py
+++ b/solution.py
@@ -10,7 +10,7 @@
 from jax.sharding import PartitionSpec as P
 
 RAYS = 32
-VMEM_BYTES = 67043328
+VMEM_BYTES = 67043328 - 2 * 1024 * 1024
 
 penalty = 1.0
 object_step = 0.1
@@ -306,6 +306,16 @@
         copy.wait_send()
 
 
+def finish(a, b, c, x, y, z, sem):
+    copies = [
+        pltpu.make_async_copy(s, t, sem.at[k]) for k, (s, t) in enumerate(((a, x), (b, y), (c, z)))
+    ]
+    for copy in copies:
+        copy.start()
+    for copy in copies:
+        copy.wait()
+
+
 def body(
     measured, positions, probe_field, object_field, dual_field, volume, radon_tiles, tile_range
 ):
@@ -321,9 +331,9 @@
     outs = pl.pallas_call(
         functools.partial(kernel, angles, strips),
         out_shape=(
-            jax.ShapeDtypeStruct((2 * columns, slices), jnp.float32),
-            jax.ShapeDtypeStruct((2 * columns, slices), jnp.float32),
-            jax.ShapeDtypeStruct((2 * pixels, slices), jnp.float32),
+            pltpu.VMEM((2 * columns, slices), jnp.float32),
+            pltpu.VMEM((2 * columns, slices), jnp.float32),
+            pltpu.VMEM((2 * pixels, slices), jnp.float32),
         ),
         in_specs=[smem, smem] + [pl.BlockSpec(memory_space=pltpu.HBM)] * 7,
         out_specs=(vmem, vmem, vmem),
@@ -364,6 +374,14 @@
         radon_tiles.reshape(angles * hit_rows, pixels),
         jnp.asarray(dft_tables(side)),
     )
+    outs = pl.pallas_call(
+        finish,
+        out_shape=[jax.ShapeDtypeStruct(o.shape, o.dtype) for o in outs],
+        in_specs=[pl.BlockSpec(memory_space=pl.ANY)] * 3,
+        out_specs=[pl.BlockSpec(memory_space=pl.ANY)] * 3,
+        scratch_shapes=[pltpu.SemaphoreType.DMA((3,))],
+        compiler_params=pltpu.CompilerParams(vmem_limit_bytes=2 * 1024 * 1024),
+    )(*outs)
     return (
         outs[0].reshape(object_field.shape),
         outs[1].reshape(dual_field.shape),

time: 46.1 us -> 42.6 us (0.924)
  local copies, waits for them, and re-layouts: 3.46 us -> 0 us
    unnamed x7 -> x0, local copies, waits for them, and re-layouts: 3.46 us -> none
    pallas_call x1 -> x2, Pallas kernels: 41.8 us -> 41.8 us  [the longest x1 40.9 us: body(): pl.pallas_call(functools.partial(kernel, angles, strips), out_shape=(pltp...]
where the time goes in v1:
time: 42.6 us; the launch traced here: 42.5 us
  Pallas kernels  41.8 us (98%)
  between operations  0.64 us (2%)
    pallas_call x1, Pallas kernels, body(): pl.pallas_call(functools.partial(kernel, angles, strips), out_shape=(pltp...  40.9 us
    pallas_call x1, Pallas kernels, body(): pl.pallas_call(finish, out_shape=[jax.ShapeDtypeStruct(o.shape, o.dtype)...  0.9 us

profile of v1, /device:TPU:0, one launch (start us, length us, event | category | flops | bytes accessed | tf_op | source)
XLA Modules:
  0.0 42.5 jit_solution(8329288826144076046)
XLA Ops:
  0.6 40.9 %shard_map.112 = (f32[512,128]{1,0:T(8,128)S(1)}, f32[512,128]{1,0:T(8,128)S(1)}, f32[512,128]{1,0:T(8,128)S(1)}) custom-call(s32[8]{0:T(128)} %bitcast.15, s32[16]{0:T(128)} %bitcast.16, f32[8,128,128]{2,1,0:T(8,128)} %bitcast.10, f32[2,128,128]{2,1,0:T(8,128)} %probe_hbm.1, f32[512,128]{1,0:T(8,128)} %bitcast.12, f32[512,128]{1,0:T(8,128)} %bitcast.13, ...), custom_call_target="tpu_custom_call" | custom-call | tf_op jit(solution)/shard_map/pallas_call | solution.py:331
  41.5 0.9 %shard_map.113 = (f32[512,128]{1,0:T(8,128)}, f32[512,128]{1,0:T(8,128)}, f32[512,128]{1,0:T(8,128)}) custom-call(f32[512,128]{1,0:T(8,128)S(1)} %get-tuple-element.9.a, f32[512,128]{1,0:T(8,128)S(1)} %get-tuple-element.10.b, f32[512,128]{1,0:T(8,128)S(1)} %get-tuple-element.11.c), custom_call_target="tpu_custom_call" | custom-call | tf_op jit(solution)/shard_map/pallas_call | solution.py:377

commit v2 on v1

v2 whole, which is shorter than its diff:
```python
import functools
import math

import jax
import jax.numpy as jnp
import numpy as np
from jax import lax
from jax.experimental import pallas as pl
from jax.experimental.pallas import tpu as pltpu
from jax.sharding import PartitionSpec as P

RAYS = 32
BLOCK = 128
VMEM_BYTES = 67043328 - 2 * 1024 * 1024

penalty = 1.0
object_step = 0.1
volume_step = 1.0
MESH = pl.DeviceIdType.MESH


def dft_tables(length):
    indices = np.arange(length, dtype=np.int64)
    angles = (indices[:, None] * indices[None, :] % length) * (2.0 * math.pi / length)
    scaling = 1.0 / math.sqrt(length)
    parts = []
    for table in (np.cos(angles) * scaling, np.sin(angles) * scaling):
        table = table.astype(np.float32)
        high = table.astype(jnp.bfloat16)
        parts += [high, (table - high.astype(np.float32)).astype(jnp.bfloat16)]
    return np.stack(parts)


def split(value):
    high = value.astype(jnp.bfloat16)
    return high, (value - high.astype(jnp.float32)).astype(jnp.bfloat16)


def dot(left, right):
    return jnp.dot(left, right, preferred_element_type=jnp.float32)


def dot3(left, right):
    return dot(left[0], right[0]) + (dot(left[0], right[1]) + dot(left[1], right[0]))


def beside(left, right):
    return jnp.concatenate([left, right], axis=1)


def above(top, low):
    return jnp.concatenate([top, low], axis=0)


def swap_blocks(value):
    half = value.shape[1] // 2
    return above(
        beside(value[:half, :half], value[half:, :half]),
        beside(value[:half, half:], value[half:, half:]),
    )


def both_parts(ref, columns):
    return beside(ref[pl.ds(0, columns, stride=2), :], ref[pl.ds(1, columns, stride=2), :])


def xor(left, right, bound):
    result, bit = 0, 1
    while bit < bound:
        result = result + ((left // bit) + (right // bit)) % 2 * bit
        bit *= 2
    return result


def kernel(
    angles, strips,
    positions, ranges, measured_hbm, probe_hbm, field_hbm, dual_hbm, volume_hbm, radon_hbm,
    tables_hbm,
    object_next, dual_next, volume_next,
    measured, probe, field, dual, volume, radon, tables,
    ray_out, ray_in, pick_out, pick_in, field_out, field_in, grad_out, grad_in,
    dense_out, dense_in, rows_half, whole_field, grads, own_grad, own_rays, turned_radon,
    load_sem, ray_send, ray_recv, pick_send, pick_recv, strip_send, strip_recv,
):
    loads = {}
    for k, (name, source, target) in enumerate((
        ("volume", volume_hbm, volume), ("radon", radon_hbm, radon), ("field", field_hbm, field),
        ("tables", tables_hbm, tables), ("probe", probe_hbm, probe),
        ("measured", measured_hbm, measured), ("dual", dual_hbm, dual),
    )):
        loads[name] = pltpu.make_async_copy(source, target, load_sem.at[k])
        loads[name].start()
    me, strip = lax.axis_index("ang"), lax.axis_index("strip")
    columns = field.shape[0] // 2
    detector = strips * columns
    frames, side = measured.shape[0], measured.shape[1]
    slices = field.shape[1]
    chunks, hit_rows = ray_out.shape[0], ray_out.shape[2]
    gap = detector - side
    if angles & (angles - 1):
        ang_peers = [lax.rem(me + offset, angles) for offset in range(1, angles)]
    else:
        ang_peers = [xor(me, offset, angles) for offset in range(angles - 1, 0, -1)]
    strip_peers = [lax.rem(strip + offset, strips) for offset in range(1, strips)]

    def rows_of(owner):
        return pl.ds(pl.multiple_of(owner * columns, columns), columns)

    barrier = pltpu.get_barrier_semaphore()
    for peer in ang_peers:
        pl.semaphore_signal(barrier, inc=1, device_id=(peer, strip), device_id_type=MESH)
    for peer in strip_peers:
        pl.semaphore_signal(barrier, inc=1, device_id=(me, peer), device_id_type=MESH)

    def remote(source, target, send, recv, device):
        return pltpu.make_async_remote_copy(
            src_ref=source, dst_ref=target, send_sem=send, recv_sem=recv,
            device_id=device, device_id_type=MESH,
        )

    others = pl.ds(0, angles - 1)
    slack = detector - hit_rows

    def window(slot):
        return pl.ds(pl.multiple_of(slack + slot * detector, RAYS), hit_rows)

    mates = pl.ds(0, strips - 1)

    def ray_copy(c, peer):
        return remote(
            ray_out.at[c, peer], ray_in[c].at[window(me)], ray_send.at[c], ray_recv.at[c],
            (peer, strip),
        )

    def ray_all(c):
        part = ray_in[c].at[pl.ds(0, (angles - 1) * hit_rows)]
        return remote(part, part, ray_send.at[c], ray_recv.at[c], (me, strip))

    def pick_copy(c, peer):
        return remote(
            pick_out.at[c, peer], pick_in.at[c, me], pick_send.at[c], pick_recv.at[c],
            (peer, strip),
        )

    def pick_all(c):
        return remote(
            pick_out.at[c, others], pick_in.at[c, others], pick_send.at[c], pick_recv.at[c],
            (me, strip),
        )

    def strip_copy(source, target, stage, peer):
        return remote(source, target, strip_send.at[stage], strip_recv.at[stage], (me, peer))

    def field_copy(peer):
        return strip_copy(field_out, field_in.at[strip], 0, peer)

    def grad_copy(c, peer):
        return strip_copy(grad_out.at[c, peer], grad_in.at[c, strip], 1 + c, peer)

    def dense_copy(c, peer):
        return strip_copy(dense_out.at[c, peer], dense_in.at[c, strip], 1 + chunks + c, peer)

    def residual_copy(c, peer):
        part = rows_half[c].at[rows_of(strip), :]
        return strip_copy(part, part, 1 + 2 * chunks + c, peer)

    def strip_all(ref, stage):
        return strip_copy(ref.at[mates], ref.at[mates], stage, strip)

    def residual_all(c):
        part = rows_half[c].at[pl.ds(0, (strips - 1) * columns), :]
        return strip_copy(part, part, 1 + 2 * chunks + c, strip)

    loads["field"].wait()
    for c in range(chunks):
        own = field[pl.ds(c, columns, stride=chunks), :]
        field_out[c] = own.astype(jnp.bfloat16)
        whole_field[c, rows_of(strip), :] = own
    loads["volume"].wait()
    pixels = volume.shape[0] // 2
    volume_half = both_parts(volume, pixels).astype(jnp.bfloat16)
    loads["radon"].wait()
    sums = dot(radon[...], volume_half).astype(jnp.bfloat16)
    for c in range(chunks):
        ray_out[c] = sums[:, c * slices:(c + 1) * slices].reshape(ray_out.shape[1:])
    pl.semaphore_wait(barrier, len(ang_peers) + len(strip_peers))
    for peer in strip_peers:
        field_copy(peer).start()
    for c in range(chunks):
        for peer in ang_peers:
            ray_copy(c, peer).start()

    for c in range(chunks):
        for p in range(angles + 1):
            ray_in[c][pl.ds(p * detector, slack), :] = jnp.zeros((slack, slices), jnp.bfloat16)
        ray_in[c][window(me), :] = ray_out[c, me]
        for j in range(frames + 1):
            grads[c, pl.ds(j * (gap + side), gap), :] = jnp.zeros((gap, slices), jnp.float32)
    turned_radon[...] = radon[...].T
    for name in ("tables", "probe", "measured", "dual"):
        loads[name].wait()
    cos_high, cos_low, sin_high, sin_low = (tables[k] for k in range(4))
    turn = tuple(
        above(beside(c, -s), beside(s, c)) for c, s in ((cos_high, sin_high), (cos_low, sin_low))
    )
    back_turn = tuple(
        above(beside(c, s), beside(-s, c)) for c, s in ((cos_high, sin_high), (cos_low, sin_low))
    )
    probe_re, probe_im = probe[0], probe[1]
    strip_all(field_in, 0).wait_recv()
    for peer in strip_peers:
        for c in range(chunks):
            whole_field[c, rows_of(peer), :] = field_in[peer, c].astype(jnp.float32)

    def frame_pair(pair):
        waves = []
        for j in (pair, pair + 1):
            re = whole_field[0, pl.ds(positions[j], side), :]
            im = whole_field[1, pl.ds(positions[j], side), :]
            waves.append(beside(probe_re * re - probe_im * im, probe_re * im + probe_im * re))
        right = dot3(split(above(*waves)), turn)
        far = dot3(back_turn, split(swap_blocks(right)))
        far_re, far_im = far[:side], far[side:]
        modulus = jnp.sqrt(far_re * far_re + far_im * far_im)
        intensity = beside(measured[pair], measured[pair + 1])
        shrink = 1.0 - jnp.sqrt(intensity) / jnp.maximum(modulus, 1.0)
        left = dot3(turn, split(above(far_re * shrink, far_im * shrink)))
        back = dot3(split(swap_blocks(left)), back_turn)
        for k in range(2):
            part = back[k * side:(k + 1) * side]
            re, im = part[:, :side], part[:, side:]
            rows = pl.ds(gap + (pair + k) * (gap + side), side)
            grads[0, rows, :] = probe_re * re + probe_im * im
            grads[1, rows, :] = probe_re * im - probe_im * re

    def deposit(c, first, rows):
        total = None
        for j in range(frames):
            start = gap + j * (gap + side) + first - positions[j]
            piece = grads[c, pl.ds(start, rows), :]
            total = piece if total is None else total + piece
        return total

    def sum_tile(c, tile):
        total = None
        for p in range(angles):
            start = ((slack + p * detector) // RAYS + tile - ranges[p]) * RAYS
            piece = ray_in[c][pl.ds(start, RAYS), :].astype(jnp.float32)
            total = piece if total is None else total + piece
        return total

    block = min(BLOCK, columns)

    def send_grads(c):
        for peer in strip_peers:
            for k in range(columns // block):
                grad_out[c, peer, pl.ds(k * block, block), :] = deposit(
                    c, peer * columns + k * block, block
                ).astype(jnp.bfloat16)
            grad_copy(c, peer).start()
        for k in range(columns // block):
            own_grad[c, pl.ds(k * block, block), :] = deposit(
                c, strip * columns + k * block, block
            )

    def send_rays(c):
        ray_all(c).wait_recv()
        tiles = columns // RAYS
        for peer in strip_peers:
            for k in range(tiles):
                dense_out[c, peer, pl.ds(k * RAYS, RAYS), :] = sum_tile(
                    c, peer * tiles + k
                ).astype(jnp.bfloat16)
            dense_copy(c, peer).start()
        for k in range(tiles):
            own_rays[c, pl.ds(k * RAYS, RAYS), :] = sum_tile(c, strip * tiles + k)

    def update(c):
        strip_all(grad_in.at[c], 1 + c).wait_recv()
        strip_all(dense_in.at[c], 1 + chunks + c).wait_recv()
        for k in range(columns // block):
            here = pl.ds(k * block, block)
            intersection, projection = own_grad[c, here, :], own_rays[c, here, :]
            for peer in strip_peers:
                intersection = intersection + grad_in[c, peer, here, :].astype(jnp.float32)
                projection = projection + dense_in[c, peer, here, :].astype(jnp.float32)
            part = pl.ds(c + k * block * chunks, block, stride=chunks)
            part_field, part_dual = field[part, :], dual[part, :]
            updated = part_field - object_step * (
                intersection + part_dual + penalty * (part_field - projection)
            )
            residual = penalty * (projection - updated) - part_dual
            rows_half[c][pl.ds(pl.multiple_of(strip * columns + k * block, block), block), :] = (
                residual.astype(jnp.bfloat16)
            )
            object_next[part, :] = updated
            dual_next[part, :] = part_dual + penalty * (updated - projection)
        for peer in strip_peers:
            residual_copy(c, peer).start()

    def send_picks(c):
        residual_all(c).wait_recv()
        for peer in ang_peers:
            pick_out[c, peer] = rows_half[c][pl.ds(ranges[peer] * RAYS, hit_rows), :]
            pick_copy(c, peer).start()
        pick_in[c, me] = rows_half[c][pl.ds(ranges[me] * RAYS, hit_rows), :]

    for pair in range(0, frames, 2):
        frame_pair(pair)
    send_grads(0)
    send_rays(0)
    for c in range(1, chunks):
        send_grads(c)
    for c in range(chunks):
        update(c)
        send_picks(c)
        if c + 1 < chunks:
            send_rays(c + 1)
    for c in range(chunks):
        pick_all(c).wait_recv()
        gradient = dot(turned_radon[...], pick_in[c].reshape(angles * hit_rows, slices))
        part = pl.ds(c, pixels, stride=chunks)
        volume_next[part, :] = volume[part, :] - volume_step * gradient
    for peer in strip_peers:
        field_copy(peer).wait_send()
    for c in range(chunks):
        ray_all(c).wait_send()
        pick_all(c).wait_send()
        strip_all(grad_out.at[c], 1 + c).wait_send()
        strip_all(dense_out.at[c], 1 + chunks + c).wait_send()
        for peer in strip_peers:
            residual_copy(c, peer).wait_send()


def finish(first, second, third, first_out, second_out, third_out, sem):
    copies = [
        pltpu.make_async_copy(source, target, sem.at[k])
        for k, (source, target) in enumerate(
            ((first, first_out), (second, second_out), (third, third_out))
        )
    ]
    for copy in copies:
        copy.start()
    for copy in copies:
        copy.wait()


def body(
    measured, positions, probe_field, object_field, dual_field, volume, radon_tiles, tile_range
):
    angles, strips = lax.axis_size("ang"), lax.axis_size("strip")
    frames, side = measured.shape[1], measured.shape[2]
    columns = object_field.shape[1]
    hit_rows = radon_tiles.shape[2] * radon_tiles.shape[3]
    pixels = radon_tiles.shape[4]
    chunks, slices = object_field.shape[2], object_field.shape[3]
    detector = strips * columns
    pad_rows = detector - side + frames * detector
    half = jnp.bfloat16
    outs = pl.pallas_call(
        functools.partial(kernel, angles, strips),
        out_shape=(
            pltpu.VMEM((chunks * columns, slices), jnp.float32),
            pltpu.VMEM((chunks * columns, slices), jnp.float32),
            pltpu.VMEM((chunks * pixels, slices), jnp.float32),
        ),
        in_specs=[pl.BlockSpec(memory_space=pltpu.SMEM)] * 2
        + [pl.BlockSpec(memory_space=pltpu.HBM)] * 7,
        out_specs=(pl.BlockSpec(memory_space=pltpu.VMEM),) * 3,
        scratch_shapes=[
            pltpu.VMEM((frames, side, side), jnp.float32),
            pltpu.VMEM((chunks, side, side), jnp.float32),
            pltpu.VMEM((chunks * columns, slices), jnp.float32),
            pltpu.VMEM((chunks * columns, slices), jnp.float32),
            pltpu.VMEM((chunks * pixels, slices), jnp.float32),
            pltpu.VMEM((angles * hit_rows, pixels), half),
            pltpu.VMEM((4, side, side), half),
            pltpu.VMEM((chunks, angles, hit_rows, slices), half),
            [pltpu.VMEM(((angles + 1) * detector - hit_rows, slices), half)] * chunks,
            pltpu.VMEM((chunks, angles, hit_rows, slices), half),
            pltpu.VMEM((chunks, angles, hit_rows, slices), half),
            pltpu.VMEM((chunks, columns, slices), half),
            pltpu.VMEM((strips, chunks, columns, slices), half),
        ] + [pltpu.VMEM((chunks, strips, columns, slices), half)] * 4 + [
            [pltpu.VMEM((detector, slices), half)] * chunks,
            pltpu.VMEM((chunks, detector, slices), jnp.float32),
            pltpu.VMEM((chunks, pad_rows, slices), jnp.float32),
            pltpu.VMEM((chunks, columns, slices), jnp.float32),
            pltpu.VMEM((chunks, columns, slices), jnp.float32),
            pltpu.VMEM((pixels, angles * hit_rows), half),
            pltpu.SemaphoreType.DMA((7,)),
        ] + [pltpu.SemaphoreType.DMA((chunks,))] * 4
        + [pltpu.SemaphoreType.DMA((1 + 3 * chunks,))] * 2,
        compiler_params=pltpu.CompilerParams(
            collective_id=0, has_side_effects=True, vmem_limit_bytes=VMEM_BYTES
        ),
    )(
        positions.reshape(frames),
        tile_range.reshape(angles),
        measured[0],
        probe_field,
        object_field.reshape(chunks * columns, slices),
        dual_field.reshape(chunks * columns, slices),
        volume.reshape(chunks * pixels, slices),
        radon_tiles.reshape(angles * hit_rows, pixels),
        jnp.asarray(dft_tables(side)),
    )
    outs = pl.pallas_call(
        finish,
        out_shape=[jax.ShapeDtypeStruct(o.shape, o.dtype) for o in outs],
        in_specs=[pl.BlockSpec(memory_space=pl.ANY)] * 3,
        out_specs=[pl.BlockSpec(memory_space=pl.ANY)] * 3,
        scratch_shapes=[pltpu.SemaphoreType.DMA((3,))],
        compiler_params=pltpu.CompilerParams(vmem_limit_bytes=2 * 1024 * 1024),
    )(*outs)
    return (
        outs[0].reshape(object_field.shape),
        outs[1].reshape(dual_field.shape),
        outs[2].reshape(volume.shape),
    )


def solution(mesh):
    return jax.shard_map(
        body,
        mesh=mesh,
        in_specs=(
            P("ang", "strip", None, None),
            P("ang", "strip"),
            P(),
            P("ang", "strip", None, None),
            P("ang", "strip", None, None),
            P(("ang", "strip"), None, None),
            P(("ang", "strip"), None, None, None, None),
            P("ang", None, "strip", None),
        ),
        out_specs=(
            P("ang", "strip", None, None),
            P("ang", "strip", None, None),
            P(("ang", "strip"), None, None),
        ),
        check_vma=False,
    )
```

time: 42.6 us -> 38.8 us (0.911)
  Pallas kernels: 41.8 us -> 38 us
    pallas_call x1, Pallas kernels: 40.9 us -> 37.1 us  [body(): pl.pallas_call(functools.partial(kernel, angles, strips), out_shape=(pltp...]
where the time goes in v2:
time: 38.8 us; the launch traced here: 38.6 us
  Pallas kernels  38 us (98%)
  between operations  0.64 us (2%)
    pallas_call x1, Pallas kernels, body(): pl.pallas_call(functools.partial(kernel, angles, strips), out_shape=(pltp...  37.1 us
    pallas_call x1, Pallas kernels, body(): pl.pallas_call(finish, out_shape=[jax.ShapeDtypeStruct(o.shape, o.dtype)...  0.9 us

profile of v2, /device:TPU:0, one launch (start us, length us, event | category | flops | bytes accessed | tf_op | source)
XLA Modules:
  0.0 38.6 jit_solution(16920492510481545768)
XLA Ops:
  0.6 37.1 %shard_map.112 = (f32[512,128]{1,0:T(8,128)S(1)}, f32[512,128]{1,0:T(8,128)S(1)}, f32[512,128]{1,0:T(8,128)S(1)}) custom-call(s32[8]{0:T(128)} %bitcast.15, s32[16]{0:T(128)} %bitcast.16, f32[8,128,128]{2,1,0:T(8,128)} %bitcast.10, f32[2,128,128]{2,1,0:T(8,128)} %probe_hbm.1, f32[512,128]{1,0:T(8,128)} %bitcast.12, f32[512,128]{1,0:T(8,128)} %bitcast.13, ...), custom_call_target="tpu_custom_call" | custom-call | tf_op jit(solution)/shard_map/pallas_call | solution.py:360
  37.7 0.9 %shard_map.113 = (f32[512,128]{1,0:T(8,128)}, f32[512,128]{1,0:T(8,128)}, f32[512,128]{1,0:T(8,128)}) custom-call(f32[512,128]{1,0:T(8,128)S(1)} %get-tuple-element.9.first, f32[512,128]{1,0:T(8,128)S(1)} %get-tuple-element.10.second, f32[512,128]{1,0:T(8,128)S(1)} %get-tuple-element.11.third), custom_call_target="tpu_custom_call" | custom-call | tf_op jit(solution)/shard_map/pallas_call | solution.py:408

commit v3 on v2

--- a/solution.py
+++ b/solution.py
@@ -10,7 +10,6 @@
 from jax.sharding import PartitionSpec as P
 
 RAYS = 32
-BLOCK = 128
 VMEM_BYTES = 67043328 - 2 * 1024 * 1024
 
 penalty = 1.0
@@ -74,17 +73,19 @@
 
 def kernel(
     angles, strips,
-    positions, ranges, measured_hbm, probe_hbm, field_hbm, dual_hbm, volume_hbm, radon_hbm,
+    positions_hbm, ranges_hbm, measured_hbm, probe_hbm, field_hbm, dual_hbm, volume_hbm, radon_hbm,
     tables_hbm,
     object_next, dual_next, volume_next,
-    measured, probe, field, dual, volume, radon, tables,
+    positions, ranges, measured, probe, field, dual, volume, radon, tables,
     ray_out, ray_in, pick_out, pick_in, field_out, field_in, grad_out, grad_in,
-    dense_out, dense_in, rows_half, whole_field, grads, own_grad, own_rays, turned_radon,
+    dense_out, dense_in, mixed_out, mixed_in, rows_half, whole_field, grads,
+    own_grad, own_rays, own_mixed, turned_radon,
     load_sem, ray_send, ray_recv, pick_send, pick_recv, strip_send, strip_recv,
 ):
     loads = {}
     for k, (name, source, target) in enumerate((
-        ("volume", volume_hbm, volume), ("radon", radon_hbm, radon), ("field", field_hbm, field),
+        ("field", field_hbm, field), ("volume", volume_hbm, volume), ("radon", radon_hbm, radon),
+        ("positions", positions_hbm, positions), ("ranges", ranges_hbm, ranges),
         ("tables", tables_hbm, tables), ("probe", probe_hbm, probe),
         ("measured", measured_hbm, measured), ("dual", dual_hbm, dual),
     )):
@@ -164,6 +165,9 @@
         part = rows_half[c].at[rows_of(strip), :]
         return strip_copy(part, part, 1 + 2 * chunks + c, peer)
 
+    def mixed_copy(c, peer):
+        return strip_copy(mixed_out.at[c, peer], mixed_in.at[c, strip], 1 + 3 * chunks + c, peer)
+
     def strip_all(ref, stage):
         return strip_copy(ref.at[mates], ref.at[mates], stage, strip)
 
@@ -176,6 +180,9 @@
         own = field[pl.ds(c, columns, stride=chunks), :]
         field_out[c] = own.astype(jnp.bfloat16)
         whole_field[c, rows_of(strip), :] = own
+    pl.semaphore_wait(barrier, len(ang_peers) + len(strip_peers))
+    for peer in strip_peers:
+        field_copy(peer).start()
     loads["volume"].wait()
     pixels = volume.shape[0] // 2
     volume_half = both_parts(volume, pixels).astype(jnp.bfloat16)
@@ -183,13 +190,12 @@
     sums = dot(radon[...], volume_half).astype(jnp.bfloat16)
     for c in range(chunks):
         ray_out[c] = sums[:, c * slices:(c + 1) * slices].reshape(ray_out.shape[1:])
-    pl.semaphore_wait(barrier, len(ang_peers) + len(strip_peers))
-    for peer in strip_peers:
-        field_copy(peer).start()
-    for c in range(chunks):
+
+    def start_rays(c):
         for peer in ang_peers:
             ray_copy(c, peer).start()
 
+    start_rays(0)
     for c in range(chunks):
         for p in range(angles + 1):
             ray_in[c][pl.ds(p * detector, slack), :] = jnp.zeros((slack, slices), jnp.bfloat16)
@@ -197,7 +203,7 @@
         for j in range(frames + 1):
             grads[c, pl.ds(j * (gap + side), gap), :] = jnp.zeros((gap, slices), jnp.float32)
     turned_radon[...] = radon[...].T
-    for name in ("tables", "probe", "measured", "dual"):
+    for name in ("positions", "ranges", "tables", "probe", "measured", "dual"):
         loads[name].wait()
     cos_high, cos_low, sin_high, sin_low = (tables[k] for k in range(4))
     turn = tuple(
@@ -249,54 +255,70 @@
             total = piece if total is None else total + piece
         return total
 
-    block = min(BLOCK, columns)
-
-    def send_grads(c):
-        for peer in strip_peers:
-            for k in range(columns // block):
-                grad_out[c, peer, pl.ds(k * block, block), :] = deposit(
-                    c, peer * columns + k * block, block
-                ).astype(jnp.bfloat16)
-            grad_copy(c, peer).start()
-        for k in range(columns // block):
-            own_grad[c, pl.ds(k * block, block), :] = deposit(
-                c, strip * columns + k * block, block
-            )
-
-    def send_rays(c):
+    tiles = columns // RAYS
+    ray_weight = penalty - penalty * penalty * object_step
+    grad_weight = penalty * object_step
+    dual_weight = 1.0 - penalty * object_step
+
+    def tile_rows(k):
+        return pl.ds(k * RAYS, RAYS)
+
+    def send_mixed(c):
         ray_all(c).wait_recv()
-        tiles = columns // RAYS
         for peer in strip_peers:
             for k in range(tiles):
-                dense_out[c, peer, pl.ds(k * RAYS, RAYS), :] = sum_tile(
-                    c, peer * tiles + k
+                rays = sum_tile(c, peer * tiles + k)
+                grad = deposit(c, peer * columns + k * RAYS, RAYS)
+                mixed_out[c, peer, tile_rows(k), :] = (
+                    ray_weight * rays + grad_weight * grad
                 ).astype(jnp.bfloat16)
+                dense_out[c, peer, tile_rows(k), :] = rays.astype(jnp.bfloat16)
+                grad_out[c, peer, tile_rows(k), :] = grad.astype(jnp.bfloat16)
+            mixed_copy(c, peer).start()
+        for k in range(tiles):
+            rays = sum_tile(c, strip * tiles + k)
+            grad = deposit(c, strip * columns + k * RAYS, RAYS)
+            part = pl.ds(c + k * RAYS * chunks, RAYS, stride=chunks)
+            own_rays[c, tile_rows(k), :] = rays
+            own_grad[c, tile_rows(k), :] = grad
+            own_mixed[c, tile_rows(k), :] = (
+                ray_weight * rays + grad_weight * grad
+                - (dual_weight * dual[part, :] + ray_weight * field[part, :])
+            )
+
+    def send_residual(c):
+        strip_all(mixed_in.at[c], 1 + 3 * chunks + c).wait_recv()
+        for k in range(tiles):
+            residual = own_mixed[c, tile_rows(k), :]
+            for peer in strip_peers:
+                residual = residual + mixed_in[c, peer, tile_rows(k), :].astype(jnp.float32)
+            rows_half[c][pl.ds(pl.multiple_of(strip * columns + k * RAYS, RAYS), RAYS), :] = (
+                residual.astype(jnp.bfloat16)
+            )
+        for peer in strip_peers:
+            residual_copy(c, peer).start()
+
+    def send_parts(c):
+        for peer in strip_peers:
+            grad_copy(c, peer).start()
             dense_copy(c, peer).start()
-        for k in range(tiles):
-            own_rays[c, pl.ds(k * RAYS, RAYS), :] = sum_tile(c, strip * tiles + k)
 
     def update(c):
         strip_all(grad_in.at[c], 1 + c).wait_recv()
         strip_all(dense_in.at[c], 1 + chunks + c).wait_recv()
-        for k in range(columns // block):
-            here = pl.ds(k * block, block)
+        for k in range(tiles):
+            here = tile_rows(k)
             intersection, projection = own_grad[c, here, :], own_rays[c, here, :]
             for peer in strip_peers:
                 intersection = intersection + grad_in[c, peer, here, :].astype(jnp.float32)
                 projection = projection + dense_in[c, peer, here, :].astype(jnp.float32)
-            part = pl.ds(c + k * block * chunks, block, stride=chunks)
+            part = pl.ds(c + k * RAYS * chunks, RAYS, stride=chunks)
             part_field, part_dual = field[part, :], dual[part, :]
             updated = part_field - object_step * (
                 intersection + part_dual + penalty * (part_field - projection)
             )
-            residual = penalty * (projection - updated) - part_dual
-            rows_half[c][pl.ds(pl.multiple_of(strip * columns + k * block, block), block), :] = (
-                residual.astype(jnp.bfloat16)
-            )
             object_next[part, :] = updated
             dual_next[part, :] = part_dual + penalty * (updated - projection)
-        for peer in strip_peers:
-            residual_copy(c, peer).start()
 
     def send_picks(c):
         residual_all(c).wait_recv()
@@ -307,15 +329,19 @@
 
     for pair in range(0, frames, 2):
         frame_pair(pair)
-    send_grads(0)
-    send_rays(0)
-    for c in range(1, chunks):
-        send_grads(c)
+        if pair == 0:
+            for c in range(1, chunks):
+                start_rays(c)
+    send_mixed(0)
+    for c in range(chunks):
+        send_residual(c)
+        if c + 1 < chunks:
+            send_mixed(c + 1)
+        send_picks(c)
+    for c in range(chunks):
+        send_parts(c)
     for c in range(chunks):
         update(c)
-        send_picks(c)
-        if c + 1 < chunks:
-            send_rays(c + 1)
     for c in range(chunks):
         pick_all(c).wait_recv()
         gradient = dot(turned_radon[...], pick_in[c].reshape(angles * hit_rows, slices))
@@ -328,6 +354,7 @@
         pick_all(c).wait_send()
         strip_all(grad_out.at[c], 1 + c).wait_send()
         strip_all(dense_out.at[c], 1 + chunks + c).wait_send()
+        strip_all(mixed_out.at[c], 1 + 3 * chunks + c).wait_send()
         for peer in strip_peers:
             residual_copy(c, peer).wait_send()
 
@@ -364,10 +391,11 @@
             pltpu.VMEM((chunks * columns, slices), jnp.float32),
             pltpu.VMEM((chunks * pixels, slices), jnp.float32),
         ),
-        in_specs=[pl.BlockSpec(memory_space=pltpu.SMEM)] * 2
-        + [pl.BlockSpec(memory_space=pltpu.HBM)] * 7,
+        in_specs=[pl.BlockSpec(memory_space=pltpu.HBM)] * 9,
         out_specs=(pl.BlockSpec(memory_space=pltpu.VMEM),) * 3,
         scratch_shapes=[
+            pltpu.SMEM((frames,), jnp.int32),
+            pltpu.SMEM((angles,), jnp.int32),
             pltpu.VMEM((frames, side, side), jnp.float32),
             pltpu.VMEM((chunks, side, side), jnp.float32),
             pltpu.VMEM((chunks * columns, slices), jnp.float32),
@@ -381,16 +409,17 @@
             pltpu.VMEM((chunks, angles, hit_rows, slices), half),
             pltpu.VMEM((chunks, columns, slices), half),
             pltpu.VMEM((strips, chunks, columns, slices), half),
-        ] + [pltpu.VMEM((chunks, strips, columns, slices), half)] * 4 + [
+        ] + [pltpu.VMEM((chunks, strips, columns, slices), half)] * 6 + [
             [pltpu.VMEM((detector, slices), half)] * chunks,
             pltpu.VMEM((chunks, detector, slices), jnp.float32),
             pltpu.VMEM((chunks, pad_rows, slices), jnp.float32),
             pltpu.VMEM((chunks, columns, slices), jnp.float32),
             pltpu.VMEM((chunks, columns, slices), jnp.float32),
+            pltpu.VMEM((chunks, columns, slices), jnp.float32),
             pltpu.VMEM((pixels, angles * hit_rows), half),
-            pltpu.SemaphoreType.DMA((7,)),
+            pltpu.SemaphoreType.DMA((9,)),
         ] + [pltpu.SemaphoreType.DMA((chunks,))] * 4
-        + [pltpu.SemaphoreType.DMA((1 + 3 * chunks,))] * 2,
+        + [pltpu.SemaphoreType.DMA((1 + 4 * chunks,))] * 2,
         compiler_params=pltpu.CompilerParams(
             collective_id=0, has_side_effects=True, vmem_limit_bytes=VMEM_BYTES
         ),

time: 38.8 us -> 36.7 us (0.946)
  Pallas kernels: 38 us -> 35.9 us
    pallas_call x1, Pallas kernels: 37.1 us -> 35 us  [body(): pl.pallas_call(functools.partial(kernel, angles, strips), out_shape=(pltp...]
where the time goes in v3:
time: 36.7 us; the launch traced here: 36.6 us
  Pallas kernels  35.9 us (98%)
  between operations  0.64 us (2%)
    pallas_call x1, Pallas kernels, body(): pl.pallas_call(functools.partial(kernel, angles, strips), out_shape=(pltp...  35 us
    pallas_call x1, Pallas kernels, body(): pl.pallas_call(finish, out_shape=[jax.ShapeDtypeStruct(o.shape, o.dtype)...  0.9 us

profile of v3, /device:TPU:0, one launch (start us, length us, event | category | flops | bytes accessed | tf_op | source)
XLA Modules:
  0.0 36.6 jit_solution(10002216242190357752)
XLA Ops:
  0.6 35.0 %shard_map.112 = (f32[512,128]{1,0:T(8,128)S(1)}, f32[512,128]{1,0:T(8,128)S(1)}, f32[512,128]{1,0:T(8,128)S(1)}) custom-call(s32[8]{0:T(128)} %bitcast.15, s32[16]{0:T(128)} %bitcast.16, f32[8,128,128]{2,1,0:T(8,128)} %bitcast.10, f32[2,128,128]{2,1,0:T(8,128)} %probe_hbm.1, f32[512,128]{1,0:T(8,128)} %bitcast.12, f32[512,128]{1,0:T(8,128)} %bitcast.13, ...), custom_call_target="tpu_custom_call" | custom-call | tf_op jit(solution)/shard_map/pallas_call | solution.py:387
  35.7 0.9 %shard_map.113 = (f32[512,128]{1,0:T(8,128)}, f32[512,128]{1,0:T(8,128)}, f32[512,128]{1,0:T(8,128)}) custom-call(f32[512,128]{1,0:T(8,128)S(1)} %get-tuple-element.9.first, f32[512,128]{1,0:T(8,128)S(1)} %get-tuple-element.10.second, f32[512,128]{1,0:T(8,128)S(1)} %get-tuple-element.11.third), custom_call_target="tpu_custom_call" | custom-call | tf_op jit(solution)/shard_map/pallas_call | solution.py:437

commit v4 on v3

--- a/solution.py
+++ b/solution.py
@@ -40,7 +40,10 @@
 
 
 def dot3(left, right):
-    return dot(left[0], right[0]) + (dot(left[0], right[1]) + dot(left[1], right[0]))
+    return dot(
+        jnp.concatenate([left[0], left[0], left[1]], axis=1),
+        jnp.concatenate([right[0], right[1], right[0]], axis=0),
+    )
 
 
 def beside(left, right):
@@ -78,7 +81,7 @@
     object_next, dual_next, volume_next,
     positions, ranges, measured, probe, field, dual, volume, radon, tables,
     ray_out, ray_in, pick_out, pick_in, field_out, field_in, grad_out, grad_in,
-    dense_out, dense_in, mixed_out, mixed_in, rows_half, whole_field, grads,
+    mixed_out, mixed_in, wide, rows_half, whole_field, grads,
     own_grad, own_rays, own_mixed, turned_radon,
     load_sem, ray_send, ray_recv, pick_send, pick_recv, strip_send, strip_recv,
 ):
@@ -158,22 +161,22 @@
     def grad_copy(c, peer):
         return strip_copy(grad_out.at[c, peer], grad_in.at[c, strip], 1 + c, peer)
 
-    def dense_copy(c, peer):
-        return strip_copy(dense_out.at[c, peer], dense_in.at[c, strip], 1 + chunks + c, peer)
-
-    def residual_copy(c, peer):
-        part = rows_half[c].at[rows_of(strip), :]
-        return strip_copy(part, part, 1 + 2 * chunks + c, peer)
-
-    def mixed_copy(c, peer):
-        return strip_copy(mixed_out.at[c, peer], mixed_in.at[c, strip], 1 + 3 * chunks + c, peer)
+    def wide_copy(c, peer):
+        part = wide.at[c, rows_of(strip), :]
+        return strip_copy(part, part, 1 + chunks + c, peer)
+
+    def mixed_copy(c, owner, peer):
+        return strip_copy(
+            mixed_out.at[c, rows_of(owner), :], mixed_in.at[c, strip, rows_of(owner), :],
+            1 + 2 * chunks + c, peer,
+        )
 
     def strip_all(ref, stage):
         return strip_copy(ref.at[mates], ref.at[mates], stage, strip)
 
-    def residual_all(c):
-        part = rows_half[c].at[pl.ds(0, (strips - 1) * columns), :]
-        return strip_copy(part, part, 1 + 2 * chunks + c, strip)
+    def wide_all(c):
+        part = wide.at[c, pl.ds(0, (strips - 1) * columns), :]
+        return strip_copy(part, part, 1 + chunks + c, strip)
 
     loads["field"].wait()
     for c in range(chunks):
@@ -187,15 +190,25 @@
     pixels = volume.shape[0] // 2
     volume_half = both_parts(volume, pixels).astype(jnp.bfloat16)
     loads["radon"].wait()
-    sums = dot(radon[...], volume_half).astype(jnp.bfloat16)
-    for c in range(chunks):
-        ray_out[c] = sums[:, c * slices:(c + 1) * slices].reshape(ray_out.shape[1:])
-
-    def start_rays(c):
-        for peer in ang_peers:
+    groups = 1 if angles & (angles - 1) or angles == 1 else 2
+    members = angles // groups
+
+    def project(group):
+        first = pl.multiple_of(group * members * hit_rows, hit_rows)
+        sums = dot(radon[pl.ds(first, members * hit_rows), :], volume_half).astype(jnp.bfloat16)
+        for c in range(chunks):
+            ray_out[c, pl.ds(group * members, members)] = (
+                sums[:, c * slices:(c + 1) * slices].reshape(members, hit_rows, slices)
+            )
+
+    def start_rays(c, peers):
+        for peer in peers:
             ray_copy(c, peer).start()
 
-    start_rays(0)
+    mine = me // members
+    for k in range(groups - 1, -1, -1):
+        project(lax.rem(mine + k, groups))
+        start_rays(0, ang_peers[:members] if k else ang_peers[(groups - 1) * members:])
     for c in range(chunks):
         for p in range(angles + 1):
             ray_in[c][pl.ds(p * detector, slack), :] = jnp.zeros((slack, slices), jnp.bfloat16)
@@ -213,7 +226,16 @@
         above(beside(c, s), beside(-s, c)) for c, s in ((cos_high, sin_high), (cos_low, sin_low))
     )
     probe_re, probe_im = probe[0], probe[1]
+    ray_weight = penalty - penalty * penalty * object_step
+    grad_weight = penalty * object_step
+    dual_weight = 1.0 - penalty * object_step
+    for c in range(chunks):
+        part = pl.ds(c, columns, stride=chunks)
+        wide[c, rows_of(strip), :] = dual_weight * dual[part, :] + ray_weight * field[part, :]
     strip_all(field_in, 0).wait_recv()
+    for c in range(chunks):
+        for peer in strip_peers:
+            wide_copy(c, peer).start()
     for peer in strip_peers:
         for c in range(chunks):
             whole_field[c, rows_of(peer), :] = field_in[peer, c].astype(jnp.float32)
@@ -256,62 +278,51 @@
         return total
 
     tiles = columns // RAYS
-    ray_weight = penalty - penalty * penalty * object_step
-    grad_weight = penalty * object_step
-    dual_weight = 1.0 - penalty * object_step
-
     def tile_rows(k):
         return pl.ds(k * RAYS, RAYS)
 
     def send_mixed(c):
         ray_all(c).wait_recv()
-        for peer in strip_peers:
+        for owner in [*strip_peers, strip]:
             for k in range(tiles):
-                rays = sum_tile(c, peer * tiles + k)
-                grad = deposit(c, peer * columns + k * RAYS, RAYS)
-                mixed_out[c, peer, tile_rows(k), :] = (
-                    ray_weight * rays + grad_weight * grad
-                ).astype(jnp.bfloat16)
-                dense_out[c, peer, tile_rows(k), :] = rays.astype(jnp.bfloat16)
-                grad_out[c, peer, tile_rows(k), :] = grad.astype(jnp.bfloat16)
-            mixed_copy(c, peer).start()
-        for k in range(tiles):
-            rays = sum_tile(c, strip * tiles + k)
-            grad = deposit(c, strip * columns + k * RAYS, RAYS)
-            part = pl.ds(c + k * RAYS * chunks, RAYS, stride=chunks)
-            own_rays[c, tile_rows(k), :] = rays
-            own_grad[c, tile_rows(k), :] = grad
-            own_mixed[c, tile_rows(k), :] = (
-                ray_weight * rays + grad_weight * grad
-                - (dual_weight * dual[part, :] + ray_weight * field[part, :])
-            )
-
-    def send_residual(c):
-        strip_all(mixed_in.at[c], 1 + 3 * chunks + c).wait_recv()
-        for k in range(tiles):
-            residual = own_mixed[c, tile_rows(k), :]
+                rays = sum_tile(c, owner * tiles + k)
+                grad = deposit(c, owner * columns + k * RAYS, RAYS)
+                mixed = ray_weight * rays + grad_weight * grad
+                rows = pl.ds(pl.multiple_of(owner * columns + k * RAYS, RAYS), RAYS)
+                own_mixed[c, rows, :] = mixed
+                mixed_out[c, rows, :] = mixed.astype(jnp.bfloat16)
+                if owner is strip:
+                    own_rays[c, tile_rows(k), :] = rays
+                    own_grad[c, tile_rows(k), :] = grad
+                else:
+                    grad_out[c, owner, tile_rows(k), :] = grad.astype(jnp.bfloat16)
+            for peer in strip_peers:
+                mixed_copy(c, owner, peer).start()
+
+    def make_residual(c):
+        wide_all(c).wait_recv()
+        strip_all(mixed_in.at[c], 1 + 2 * chunks + c).wait_recv()
+        for k in range(detector // RAYS):
+            residual = own_mixed[c, tile_rows(k), :] - wide[c, tile_rows(k), :]
             for peer in strip_peers:
                 residual = residual + mixed_in[c, peer, tile_rows(k), :].astype(jnp.float32)
-            rows_half[c][pl.ds(pl.multiple_of(strip * columns + k * RAYS, RAYS), RAYS), :] = (
-                residual.astype(jnp.bfloat16)
-            )
-        for peer in strip_peers:
-            residual_copy(c, peer).start()
+            rows_half[c][tile_rows(k), :] = residual.astype(jnp.bfloat16)
 
     def send_parts(c):
         for peer in strip_peers:
             grad_copy(c, peer).start()
-            dense_copy(c, peer).start()
 
     def update(c):
         strip_all(grad_in.at[c], 1 + c).wait_recv()
-        strip_all(dense_in.at[c], 1 + chunks + c).wait_recv()
         for k in range(tiles):
             here = tile_rows(k)
+            own_tile = pl.ds(pl.multiple_of(strip * columns + k * RAYS, RAYS), RAYS)
             intersection, projection = own_grad[c, here, :], own_rays[c, here, :]
             for peer in strip_peers:
-                intersection = intersection + grad_in[c, peer, here, :].astype(jnp.float32)
-                projection = projection + dense_in[c, peer, here, :].astype(jnp.float32)
+                grad = grad_in[c, peer, here, :].astype(jnp.float32)
+                mixed = mixed_in[c, peer, own_tile, :].astype(jnp.float32)
+                intersection = intersection + grad
+                projection = projection + (mixed - grad_weight * grad) * (1.0 / ray_weight)
             part = pl.ds(c + k * RAYS * chunks, RAYS, stride=chunks)
             part_field, part_dual = field[part, :], dual[part, :]
             updated = part_field - object_step * (
@@ -321,7 +332,7 @@
             dual_next[part, :] = part_dual + penalty * (updated - projection)
 
     def send_picks(c):
-        residual_all(c).wait_recv()
+        make_residual(c)
         for peer in ang_peers:
             pick_out[c, peer] = rows_half[c][pl.ds(ranges[peer] * RAYS, hit_rows), :]
             pick_copy(c, peer).start()
@@ -329,14 +340,11 @@
 
     for pair in range(0, frames, 2):
         frame_pair(pair)
-        if pair == 0:
+        if pair == 2:
             for c in range(1, chunks):
-                start_rays(c)
-    send_mixed(0)
-    for c in range(chunks):
-        send_residual(c)
-        if c + 1 < chunks:
-            send_mixed(c + 1)
+                start_rays(c, ang_peers)
+    for c in range(chunks):
+        send_mixed(c)
         send_picks(c)
     for c in range(chunks):
         send_parts(c)
@@ -353,10 +361,9 @@
         ray_all(c).wait_send()
         pick_all(c).wait_send()
         strip_all(grad_out.at[c], 1 + c).wait_send()
-        strip_all(dense_out.at[c], 1 + chunks + c).wait_send()
-        strip_all(mixed_out.at[c], 1 + 3 * chunks + c).wait_send()
+        strip_all(mixed_in.at[c], 1 + 2 * chunks + c).wait_send()
         for peer in strip_peers:
-            residual_copy(c, peer).wait_send()
+            wide_copy(c, peer).wait_send()
 
 
 def finish(first, second, third, first_out, second_out, third_out, sem):
@@ -409,17 +416,20 @@
             pltpu.VMEM((chunks, angles, hit_rows, slices), half),
             pltpu.VMEM((chunks, columns, slices), half),
             pltpu.VMEM((strips, chunks, columns, slices), half),
-        ] + [pltpu.VMEM((chunks, strips, columns, slices), half)] * 6 + [
+        ] + [pltpu.VMEM((chunks, strips, columns, slices), half)] * 2 + [
+            pltpu.VMEM((chunks, detector, slices), half),
+            pltpu.VMEM((chunks, strips, detector, slices), half),
+            pltpu.VMEM((chunks, detector, slices), jnp.float32),
             [pltpu.VMEM((detector, slices), half)] * chunks,
             pltpu.VMEM((chunks, detector, slices), jnp.float32),
             pltpu.VMEM((chunks, pad_rows, slices), jnp.float32),
             pltpu.VMEM((chunks, columns, slices), jnp.float32),
             pltpu.VMEM((chunks, columns, slices), jnp.float32),
-            pltpu.VMEM((chunks, columns, slices), jnp.float32),
+            pltpu.VMEM((chunks, detector, slices), jnp.float32),
             pltpu.VMEM((pixels, angles * hit_rows), half),
             pltpu.SemaphoreType.DMA((9,)),
         ] + [pltpu.SemaphoreType.DMA((chunks,))] * 4
-        + [pltpu.SemaphoreType.DMA((1 + 4 * chunks,))] * 2,
+        + [pltpu.SemaphoreType.DMA((1 + 3 * chunks,))] * 2,
         compiler_params=pltpu.CompilerParams(
             collective_id=0, has_side_effects=True, vmem_limit_bytes=VMEM_BYTES
         ),

time: 36.7 us -> 35.2 us (0.959)
  Pallas kernels: 35.9 us -> 34.4 us
    pallas_call x1, Pallas kernels: 35 us -> 33.5 us  [body(): pl.pallas_call(functools.partial(kernel, angles, strips), out_shape=(pltp...]
where the time goes in v4:
time: 35.2 us; the launch traced here: 35 us
  Pallas kernels  34.4 us (98%)
  between operations  0.64 us (2%)
    pallas_call x1, Pallas kernels, body(): pl.pallas_call(functools.partial(kernel, angles, strips), out_shape=(pltp...  33.5 us
    pallas_call x1, Pallas kernels, body(): pl.pallas_call(finish, out_shape=[jax.ShapeDtypeStruct(o.shape, o.dtype)...  0.9 us

profile of v4, /device:TPU:0, one launch (start us, length us, event | category | flops | bytes accessed | tf_op | source)
XLA Modules:
  0.0 35.0 jit_solution(3314280103993090743)
XLA Ops:
  0.6 33.5 %shard_map.112 = (f32[512,128]{1,0:T(8,128)S(1)}, f32[512,128]{1,0:T(8,128)S(1)}, f32[512,128]{1,0:T(8,128)S(1)}) custom-call(s32[8]{0:T(128)} %bitcast.15, s32[16]{0:T(128)} %bitcast.16, f32[8,128,128]{2,1,0:T(8,128)} %bitcast.10, f32[2,128,128]{2,1,0:T(8,128)} %probe_hbm.1, f32[512,128]{1,0:T(8,128)} %bitcast.12, f32[512,128]{1,0:T(8,128)} %bitcast.13, ...), custom_call_target="tpu_custom_call" | custom-call | tf_op jit(solution)/shard_map/pallas_call | solution.py:394
  34.1 0.9 %shard_map.113 = (f32[512,128]{1,0:T(8,128)}, f32[512,128]{1,0:T(8,128)}, f32[512,128]{1,0:T(8,128)}) custom-call(f32[512,128]{1,0:T(8,128)S(1)} %get-tuple-element.9.first, f32[512,128]{1,0:T(8,128)S(1)} %get-tuple-element.10.second, f32[512,128]{1,0:T(8,128)S(1)} %get-tuple-element.11.third), custom_call_target="tpu_custom_call" | custom-call | tf_op jit(solution)/shard_map/pallas_call | solution.py:447

commit v5 on v4

--- a/solution.py
+++ b/solution.py
@@ -10,6 +10,7 @@
 from jax.sharding import PartitionSpec as P
 
 RAYS = 32
+BLOCK = 128
 VMEM_BYTES = 67043328 - 2 * 1024 * 1024
 
 penalty = 1.0
@@ -101,10 +102,23 @@
     slices = field.shape[1]
     chunks, hit_rows = ray_out.shape[0], ray_out.shape[2]
     gap = detector - side
-    if angles & (angles - 1):
+    if angles & (angles - 1) or angles < 4:
+        groups, members, edge = 1, angles, me >= 0
         ang_peers = [lax.rem(me + offset, angles) for offset in range(1, angles)]
+        far_peers = []
     else:
-        ang_peers = [xor(me, offset, angles) for offset in range(angles - 1, 0, -1)]
+        groups, members, quarter = 2, angles // 2, angles // 4
+        plane, low = me // quarter, lax.rem(me, quarter)
+        side_of = me // members
+        edge = (plane + 1) // 2 * 2 != 2
+        mates = [xor(low, j, quarter) for j in range(quarter - 1, -1, -1)]
+        ang_peers = [
+            there * quarter + mate
+            for there in (3 - 3 * side_of, 2 - side_of, 4 * side_of + 1 - plane)
+            for mate in mates
+        ] + [plane * quarter + mate for mate in mates[:-1]]
+        far_peers = ang_peers[:members]
+    near_peers = ang_peers[len(far_peers):]
     strip_peers = [lax.rem(strip + offset, strips) for offset in range(1, strips)]
 
     def rows_of(owner):
@@ -128,7 +142,7 @@
     def window(slot):
         return pl.ds(pl.multiple_of(slack + slot * detector, RAYS), hit_rows)
 
-    mates = pl.ds(0, strips - 1)
+    rest = pl.ds(0, strips - 1)
 
     def ray_copy(c, peer):
         return remote(
@@ -172,7 +186,7 @@
         )
 
     def strip_all(ref, stage):
-        return strip_copy(ref.at[mates], ref.at[mates], stage, strip)
+        return strip_copy(ref.at[rest], ref.at[rest], stage, strip)
 
     def wide_all(c):
         part = wide.at[c, pl.ds(0, (strips - 1) * columns), :]
@@ -183,16 +197,10 @@
         own = field[pl.ds(c, columns, stride=chunks), :]
         field_out[c] = own.astype(jnp.bfloat16)
         whole_field[c, rows_of(strip), :] = own
-    pl.semaphore_wait(barrier, len(ang_peers) + len(strip_peers))
-    for peer in strip_peers:
-        field_copy(peer).start()
     loads["volume"].wait()
     pixels = volume.shape[0] // 2
     volume_half = both_parts(volume, pixels).astype(jnp.bfloat16)
     loads["radon"].wait()
-    groups = 1 if angles & (angles - 1) or angles == 1 else 2
-    members = angles // groups
-
     def project(group):
         first = pl.multiple_of(group * members * hit_rows, hit_rows)
         sums = dot(radon[pl.ds(first, members * hit_rows), :], volume_half).astype(jnp.bfloat16)
@@ -206,9 +214,20 @@
             ray_copy(c, peer).start()
 
     mine = me // members
-    for k in range(groups - 1, -1, -1):
-        project(lax.rem(mine + k, groups))
-        start_rays(0, ang_peers[:members] if k else ang_peers[(groups - 1) * members:])
+    project(lax.rem(mine + groups - 1, groups))
+    pl.semaphore_wait(barrier, len(ang_peers) + len(strip_peers))
+    for peer in strip_peers:
+        field_copy(peer).start()
+    start_rays(0, far_peers)
+    if groups > 1:
+        project(mine)
+    start_rays(0, near_peers)
+
+    @pl.when(jnp.logical_not(edge))
+    def _():
+        for c in range(1, chunks):
+            start_rays(c, ang_peers)
+
     for c in range(chunks):
         for p in range(angles + 1):
             ray_in[c][pl.ds(p * detector, slack), :] = jnp.zeros((slack, slices), jnp.bfloat16)
@@ -269,33 +288,34 @@
             total = piece if total is None else total + piece
         return total
 
-    def sum_tile(c, tile):
+    def sum_rays(c, first, rows):
         total = None
         for p in range(angles):
-            start = ((slack + p * detector) // RAYS + tile - ranges[p]) * RAYS
-            piece = ray_in[c][pl.ds(start, RAYS), :].astype(jnp.float32)
+            start = ((slack + p * detector + first) // RAYS - ranges[p]) * RAYS
+            piece = ray_in[c][pl.ds(start, rows), :].astype(jnp.float32)
             total = piece if total is None else total + piece
         return total
 
-    tiles = columns // RAYS
+    tiles, block = columns // RAYS, math.gcd(BLOCK, columns)
+
     def tile_rows(k):
         return pl.ds(k * RAYS, RAYS)
 
     def send_mixed(c):
         ray_all(c).wait_recv()
         for owner in [*strip_peers, strip]:
-            for k in range(tiles):
-                rays = sum_tile(c, owner * tiles + k)
-                grad = deposit(c, owner * columns + k * RAYS, RAYS)
+            for k in range(0, columns, block):
+                first = pl.multiple_of(owner * columns + k, block)
+                rays = sum_rays(c, first, block)
+                grad = deposit(c, first, block)
                 mixed = ray_weight * rays + grad_weight * grad
-                rows = pl.ds(pl.multiple_of(owner * columns + k * RAYS, RAYS), RAYS)
-                own_mixed[c, rows, :] = mixed
-                mixed_out[c, rows, :] = mixed.astype(jnp.bfloat16)
+                own_mixed[c, pl.ds(first, block), :] = mixed
+                mixed_out[c, pl.ds(first, block), :] = mixed.astype(jnp.bfloat16)
                 if owner is strip:
-                    own_rays[c, tile_rows(k), :] = rays
-                    own_grad[c, tile_rows(k), :] = grad
+                    own_rays[c, pl.ds(k, block), :] = rays
+                    own_grad[c, pl.ds(k, block), :] = grad
                 else:
-                    grad_out[c, owner, tile_rows(k), :] = grad.astype(jnp.bfloat16)
+                    grad_out[c, owner, pl.ds(k, block), :] = grad.astype(jnp.bfloat16)
             for peer in strip_peers:
                 mixed_copy(c, owner, peer).start()
 
@@ -340,9 +360,13 @@
 
     for pair in range(0, frames, 2):
         frame_pair(pair)
-        if pair == 2:
-            for c in range(1, chunks):
-                start_rays(c, ang_peers)
+        if pair == 0:
+
+            @pl.when(edge)
+            def _():
+                for c in range(1, chunks):
+                    start_rays(c, ang_peers)
+
     for c in range(chunks):
         send_mixed(c)
         send_picks(c)

time: 35.2 us -> 33.6 us (0.955)
  Pallas kernels: 34.4 us -> 32.8 us
    pallas_call x1, Pallas kernels: 33.5 us -> 31.9 us  [body(): pl.pallas_call(functools.partial(kernel, angles, strips), out_shape=(pltp...]
where the time goes in v5:
time: 33.6 us; the launch traced here: 33.4 us
  Pallas kernels  32.8 us (98%)
  between operations  0.64 us (2%)
    pallas_call x1, Pallas kernels, body(): pl.pallas_call(functools.partial(kernel, angles, strips), out_shape=(pltp...  31.9 us
    pallas_call x1, Pallas kernels, body(): pl.pallas_call(finish, out_shape=[jax.ShapeDtypeStruct(o.shape, o.dtype)...  0.9 us

profile of v5, /device:TPU:0, one launch (start us, length us, event | category | flops | bytes accessed | tf_op | source)
XLA Modules:
  0.0 33.4 jit_solution(15215895297997576941)
XLA Ops:
  0.6 31.9 %shard_map.112 = (f32[512,128]{1,0:T(8,128)S(1)}, f32[512,128]{1,0:T(8,128)S(1)}, f32[512,128]{1,0:T(8,128)S(1)}) custom-call(s32[8]{0:T(128)} %bitcast.15, s32[16]{0:T(128)} %bitcast.16, f32[8,128,128]{2,1,0:T(8,128)} %bitcast.10, f32[2,128,128]{2,1,0:T(8,128)} %probe_hbm.1, f32[512,128]{1,0:T(8,128)} %bitcast.12, f32[512,128]{1,0:T(8,128)} %bitcast.13, ...), custom_call_target="tpu_custom_call" | custom-call | tf_op jit(solution)/shard_map/pallas_call | solution.py:418
  32.5 0.9 %shard_map.113 = (f32[512,128]{1,0:T(8,128)}, f32[512,128]{1,0:T(8,128)}, f32[512,128]{1,0:T(8,128)}) custom-call(f32[512,128]{1,0:T(8,128)S(1)} %get-tuple-element.9.first, f32[512,128]{1,0:T(8,128)S(1)} %get-tuple-element.10.second, f32[512,128]{1,0:T(8,128)S(1)} %get-tuple-element.11.third), custom_call_target="tpu_custom_call" | custom-call | tf_op jit(solution)/shard_map/pallas_call | solution.py:471

commit v6 on v5

--- a/solution.py
+++ b/solution.py
@@ -47,6 +47,10 @@
     )
 
 
+def dot2(left, right):
+    return dot(jnp.concatenate([left[0], left[1]], axis=1), jnp.concatenate([right, right], axis=0))
+
+
 def beside(left, right):
     return jnp.concatenate([left, right], axis=1)
 
@@ -82,16 +86,16 @@
     object_next, dual_next, volume_next,
     positions, ranges, measured, probe, field, dual, volume, radon, tables,
     ray_out, ray_in, pick_out, pick_in, field_out, field_in, grad_out, grad_in,
-    mixed_out, mixed_in, wide, rows_half, whole_field, grads,
+    mixed_out, mixed_in, wide_out, wide_in, rows_half, whole_field, grads,
     own_grad, own_rays, own_mixed, turned_radon,
     load_sem, ray_send, ray_recv, pick_send, pick_recv, strip_send, strip_recv,
 ):
     loads = {}
     for k, (name, source, target) in enumerate((
         ("field", field_hbm, field), ("volume", volume_hbm, volume), ("radon", radon_hbm, radon),
-        ("positions", positions_hbm, positions), ("ranges", ranges_hbm, ranges),
+        ("dual", dual_hbm, dual), ("positions", positions_hbm, positions), ("ranges", ranges_hbm, ranges),
         ("tables", tables_hbm, tables), ("probe", probe_hbm, probe),
-        ("measured", measured_hbm, measured), ("dual", dual_hbm, dual),
+        ("measured", measured_hbm, measured),
     )):
         loads[name] = pltpu.make_async_copy(source, target, load_sem.at[k])
         loads[name].start()
@@ -176,8 +180,7 @@
         return strip_copy(grad_out.at[c, peer], grad_in.at[c, strip], 1 + c, peer)
 
     def wide_copy(c, peer):
-        part = wide.at[c, rows_of(strip), :]
-        return strip_copy(part, part, 1 + chunks + c, peer)
+        return strip_copy(wide_out[c], wide_in[c].at[strip], 1 + chunks + c, peer)
 
     def mixed_copy(c, owner, peer):
         return strip_copy(
@@ -187,10 +190,6 @@
 
     def strip_all(ref, stage):
         return strip_copy(ref.at[rest], ref.at[rest], stage, strip)
-
-    def wide_all(c):
-        part = wide.at[c, pl.ds(0, (strips - 1) * columns), :]
-        return strip_copy(part, part, 1 + chunks + c, strip)
 
     loads["field"].wait()
     for c in range(chunks):
@@ -215,6 +214,16 @@
 
     mine = me // members
     project(lax.rem(mine + groups - 1, groups))
+    loads["dual"].wait()
+    ray_weight = penalty - penalty * penalty * object_step
+    grad_weight = penalty * object_step
+    dual_weight = 1.0 - penalty * object_step
+    for c in range(chunks):
+        part = pl.ds(c, columns, stride=chunks)
+        below = field[part, :] - field_out[c].astype(jnp.float32)
+        wide_out[c][...] = (dual_weight * dual[part, :] + ray_weight * below).astype(
+            wide_out[c].dtype
+        )
     pl.semaphore_wait(barrier, len(ang_peers) + len(strip_peers))
     for peer in strip_peers:
         field_copy(peer).start()
@@ -222,6 +231,9 @@
     if groups > 1:
         project(mine)
     start_rays(0, near_peers)
+    for c in range(chunks):
+        for peer in strip_peers:
+            wide_copy(c, peer).start()
 
     @pl.when(jnp.logical_not(edge))
     def _():
@@ -235,7 +247,7 @@
         for j in range(frames + 1):
             grads[c, pl.ds(j * (gap + side), gap), :] = jnp.zeros((gap, slices), jnp.float32)
     turned_radon[...] = radon[...].T
-    for name in ("positions", "ranges", "tables", "probe", "measured", "dual"):
+    for name in ("positions", "ranges", "tables", "probe", "measured"):
         loads[name].wait()
     cos_high, cos_low, sin_high, sin_low = (tables[k] for k in range(4))
     turn = tuple(
@@ -245,16 +257,7 @@
         above(beside(c, s), beside(-s, c)) for c, s in ((cos_high, sin_high), (cos_low, sin_low))
     )
     probe_re, probe_im = probe[0], probe[1]
-    ray_weight = penalty - penalty * penalty * object_step
-    grad_weight = penalty * object_step
-    dual_weight = 1.0 - penalty * object_step
-    for c in range(chunks):
-        part = pl.ds(c, columns, stride=chunks)
-        wide[c, rows_of(strip), :] = dual_weight * dual[part, :] + ray_weight * field[part, :]
     strip_all(field_in, 0).wait_recv()
-    for c in range(chunks):
-        for peer in strip_peers:
-            wide_copy(c, peer).start()
     for peer in strip_peers:
         for c in range(chunks):
             whole_field[c, rows_of(peer), :] = field_in[peer, c].astype(jnp.float32)
@@ -271,8 +274,10 @@
         modulus = jnp.sqrt(far_re * far_re + far_im * far_im)
         intensity = beside(measured[pair], measured[pair + 1])
         shrink = 1.0 - jnp.sqrt(intensity) / jnp.maximum(modulus, 1.0)
-        left = dot3(turn, split(above(far_re * shrink, far_im * shrink)))
-        back = dot3(split(swap_blocks(left)), back_turn)
+        left = dot2(turn, above(far_re * shrink, far_im * shrink).astype(jnp.bfloat16))
+        back = dot(
+            beside(*[swap_blocks(left).astype(jnp.bfloat16)] * 2), above(*back_turn)
+        )
         for k in range(2):
             part = back[k * side:(k + 1) * side]
             re, im = part[:, :side], part[:, side:]
@@ -320,13 +325,20 @@
                 mixed_copy(c, owner, peer).start()
 
     def make_residual(c):
-        wide_all(c).wait_recv()
+        strip_all(wide_in[c], 1 + chunks + c).wait_recv()
         strip_all(mixed_in.at[c], 1 + 2 * chunks + c).wait_recv()
-        for k in range(detector // RAYS):
-            residual = own_mixed[c, tile_rows(k), :] - wide[c, tile_rows(k), :]
-            for peer in strip_peers:
-                residual = residual + mixed_in[c, peer, tile_rows(k), :].astype(jnp.float32)
-            rows_half[c][tile_rows(k), :] = residual.astype(jnp.bfloat16)
+        for owner in [*strip_peers, strip]:
+            for k in range(tiles):
+                rows = pl.ds(pl.multiple_of(owner * columns + k * RAYS, RAYS), RAYS)
+                residual = own_mixed[c, rows, :] - ray_weight * whole_field[c, rows, :]
+                if owner is strip:
+                    part = pl.ds(c + k * RAYS * chunks, RAYS, stride=chunks)
+                    residual = residual - dual_weight * dual[part, :]
+                else:
+                    residual = residual - wide_in[c][owner, tile_rows(k), :].astype(jnp.float32)
+                for peer in strip_peers:
+                    residual = residual + mixed_in[c, peer, rows, :].astype(jnp.float32)
+                rows_half[c][rows, :] = residual.astype(jnp.bfloat16)
 
     def send_parts(c):
         for peer in strip_peers:
@@ -415,6 +427,7 @@
     detector = strips * columns
     pad_rows = detector - side + frames * detector
     half = jnp.bfloat16
+    wide_kinds = [half] + [jnp.float32] * (chunks - 1)
     outs = pl.pallas_call(
         functools.partial(kernel, angles, strips),
         out_shape=(
@@ -443,7 +456,8 @@
         ] + [pltpu.VMEM((chunks, strips, columns, slices), half)] * 2 + [
             pltpu.VMEM((chunks, detector, slices), half),
             pltpu.VMEM((chunks, strips, detector, slices), half),
-            pltpu.VMEM((chunks, detector, slices), jnp.float32),
+            [pltpu.VMEM((columns, slices), kind) for kind in wide_kinds],
+            [pltpu.VMEM((strips, columns, slices), kind) for kind in wide_kinds],
             [pltpu.VMEM((detector, slices), half)] * chunks,
             pltpu.VMEM((chunks, detector, slices), jnp.float32),
             pltpu.VMEM((chunks, pad_rows, slices), jnp.float32),

time: 33.6 us -> 32.5 us (0.967)
  Pallas kernels: 32.8 us -> 31.7 us
    pallas_call x1, Pallas kernels: 31.9 us -> 30.8 us  [body(): pl.pallas_call(functools.partial(kernel, angles, strips), out_shape=(pltp...]
where the time goes in v6:
time: 32.5 us; the launch traced here: 32.3 us
  Pallas kernels  31.7 us (98%)
  between operations  0.64 us (2%)
    pallas_call x1, Pallas kernels, body(): pl.pallas_call(functools.partial(kernel, angles, strips), out_shape=(pltp...  30.8 us
    pallas_call x1, Pallas kernels, body(): pl.pallas_call(finish, out_shape=[jax.ShapeDtypeStruct(o.shape, o.dtype)...  0.9 us

profile of v6, /device:TPU:0, one launch (start us, length us, event | category | flops | bytes accessed | tf_op | source)
XLA Modules:
  0.0 32.3 jit_solution(14224297277877624721)
XLA Ops:
  0.6 30.8 %shard_map.112 = (f32[512,128]{1,0:T(8,128)S(1)}, f32[512,128]{1,0:T(8,128)S(1)}, f32[512,128]{1,0:T(8,128)S(1)}) custom-call(s32[8]{0:T(128)} %bitcast.15, s32[16]{0:T(128)} %bitcast.16, f32[8,128,128]{2,1,0:T(8,128)} %bitcast.10, f32[2,128,128]{2,1,0:T(8,128)} %probe_hbm.1, f32[512,128]{1,0:T(8,128)} %bitcast.12, f32[512,128]{1,0:T(8,128)} %bitcast.13, ...), custom_call_target="tpu_custom_call" | custom-call | tf_op jit(solution)/shard_map/pallas_call | solution.py:431
  31.4 0.9 %shard_map.113 = (f32[512,128]{1,0:T(8,128)}, f32[512,128]{1,0:T(8,128)}, f32[512,128]{1,0:T(8,128)}) custom-call(f32[512,128]{1,0:T(8,128)S(1)} %get-tuple-element.9.first, f32[512,128]{1,0:T(8,128)S(1)} %get-tuple-element.10.second, f32[512,128]{1,0:T(8,128)S(1)} %get-tuple-element.11.third), custom_call_target="tpu_custom_call" | custom-call | tf_op jit(solution)/shard_map/pallas_call | solution.py:485

commit v7 on v6

--- a/solution.py
+++ b/solution.py
@@ -90,16 +90,22 @@
     own_grad, own_rays, own_mixed, turned_radon,
     load_sem, ray_send, ray_recv, pick_send, pick_recv, strip_send, strip_recv,
 ):
+    me, strip = lax.axis_index("ang"), lax.axis_index("strip")
+    half_rows = radon.shape[0] // 2
+    far_half = (me // (angles // 2) + 1) % 2
+    far_rows = pl.ds(pl.multiple_of(far_half * half_rows, half_rows), half_rows)
+    near_rows = pl.ds(pl.multiple_of((1 - far_half) * half_rows, half_rows), half_rows)
     loads = {}
     for k, (name, source, target) in enumerate((
-        ("field", field_hbm, field), ("volume", volume_hbm, volume), ("radon", radon_hbm, radon),
+        ("field", field_hbm, field), ("volume", volume_hbm, volume),
+        ("radon_far", radon_hbm.at[far_rows], radon.at[far_rows]),
+        ("radon_near", radon_hbm.at[near_rows], radon.at[near_rows]),
         ("dual", dual_hbm, dual), ("positions", positions_hbm, positions), ("ranges", ranges_hbm, ranges),
         ("tables", tables_hbm, tables), ("probe", probe_hbm, probe),
         ("measured", measured_hbm, measured),
     )):
         loads[name] = pltpu.make_async_copy(source, target, load_sem.at[k])
         loads[name].start()
-    me, strip = lax.axis_index("ang"), lax.axis_index("strip")
     columns = field.shape[0] // 2
     detector = strips * columns
     frames, side = measured.shape[0], measured.shape[1]
@@ -199,7 +205,9 @@
     loads["volume"].wait()
     pixels = volume.shape[0] // 2
     volume_half = both_parts(volume, pixels).astype(jnp.bfloat16)
-    loads["radon"].wait()
+    loads["radon_far"].wait()
+    if angles & (angles - 1) or angles < 4:
+        loads["radon_near"].wait()
     def project(group):
         first = pl.multiple_of(group * members * hit_rows, hit_rows)
         sums = dot(radon[pl.ds(first, members * hit_rows), :], volume_half).astype(jnp.bfloat16)
@@ -214,31 +222,27 @@
 
     mine = me // members
     project(lax.rem(mine + groups - 1, groups))
-    loads["dual"].wait()
-    ray_weight = penalty - penalty * penalty * object_step
-    grad_weight = penalty * object_step
-    dual_weight = 1.0 - penalty * object_step
-    for c in range(chunks):
-        part = pl.ds(c, columns, stride=chunks)
-        below = field[part, :] - field_out[c].astype(jnp.float32)
-        wide_out[c][...] = (dual_weight * dual[part, :] + ray_weight * below).astype(
-            wide_out[c].dtype
-        )
     pl.semaphore_wait(barrier, len(ang_peers) + len(strip_peers))
     for peer in strip_peers:
         field_copy(peer).start()
     start_rays(0, far_peers)
     if groups > 1:
+        loads["radon_near"].wait()
         project(mine)
     start_rays(0, near_peers)
+    loads["dual"].wait()
+    ray_weight = penalty - penalty * penalty * object_step
+    grad_weight = penalty * object_step
+    dual_weight = 1.0 - penalty * object_step
+    for c in range(chunks):
+        part = pl.ds(c, columns, stride=chunks)
+        below = field[part, :] - field_out[c].astype(jnp.float32)
+        wide_out[c][...] = (dual_weight * dual[part, :] + ray_weight * below).astype(
+            wide_out[c].dtype
+        )
     for c in range(chunks):
         for peer in strip_peers:
             wide_copy(c, peer).start()
-
-    @pl.when(jnp.logical_not(edge))
-    def _():
-        for c in range(1, chunks):
-            start_rays(c, ang_peers)
 
     for c in range(chunks):
         for p in range(angles + 1):
@@ -373,11 +377,8 @@
     for pair in range(0, frames, 2):
         frame_pair(pair)
         if pair == 0:
-
-            @pl.when(edge)
-            def _():
-                for c in range(1, chunks):
-                    start_rays(c, ang_peers)
+            for c in range(1, chunks):
+                start_rays(c, ang_peers)
 
     for c in range(chunks):
         send_mixed(c)
@@ -465,7 +466,7 @@
             pltpu.VMEM((chunks, columns, slices), jnp.float32),
             pltpu.VMEM((chunks, detector, slices), jnp.float32),
             pltpu.VMEM((pixels, angles * hit_rows), half),
-            pltpu.SemaphoreType.DMA((9,)),
+            pltpu.SemaphoreType.DMA((10,)),
         ] + [pltpu.SemaphoreType.DMA((chunks,))] * 4
         + [pltpu.SemaphoreType.DMA((1 + 3 * chunks,))] * 2,
         compiler_params=pltpu.CompilerParams(

time: 32.5 us -> 32.4 us (level)
  no operation moved by 1% of the time
where the time goes in v7:
time: 32.4 us; the launch traced here: 32.3 us
  Pallas kernels  31.6 us (98%)
  between operations  0.64 us (2%)
    pallas_call x1, Pallas kernels, body(): pl.pallas_call(functools.partial(kernel, angles, strips), out_shape=(pltp...  30.7 us
    pallas_call x1, Pallas kernels, body(): pl.pallas_call(finish, out_shape=[jax.ShapeDtypeStruct(o.shape, o.dtype)...  0.9 us

profile of v7, /device:TPU:0, one launch (start us, length us, event | category | flops | bytes accessed | tf_op | source)
XLA Modules:
  0.0 32.3 jit_solution(4138856088838414249)
XLA Ops:
  0.6 30.7 %shard_map.112 = (f32[512,128]{1,0:T(8,128)S(1)}, f32[512,128]{1,0:T(8,128)S(1)}, f32[512,128]{1,0:T(8,128)S(1)}) custom-call(s32[8]{0:T(128)} %bitcast.15, s32[16]{0:T(128)} %bitcast.16, f32[8,128,128]{2,1,0:T(8,128)} %bitcast.10, f32[2,128,128]{2,1,0:T(8,128)} %probe_hbm.1, f32[512,128]{1,0:T(8,128)} %bitcast.12, f32[512,128]{1,0:T(8,128)} %bitcast.13, ...), custom_call_target="tpu_custom_call" | custom-call | tf_op jit(solution)/shard_map/pallas_call | solution.py:432
  31.4 0.9 %shard_map.113 = (f32[512,128]{1,0:T(8,128)}, f32[512,128]{1,0:T(8,128)}, f32[512,128]{1,0:T(8,128)}) custom-call(f32[512,128]{1,0:T(8,128)S(1)} %get-tuple-element.9.first, f32[512,128]{1,0:T(8,128)S(1)} %get-tuple-element.10.second, f32[512,128]{1,0:T(8,128)S(1)} %get-tuple-element.11.third), custom_call_target="tpu_custom_call" | custom-call | tf_op jit(solution)/shard_map/pallas_call | solution.py:486

commit v8 on v6

--- a/solution.py
+++ b/solution.py
@@ -158,15 +158,18 @@
         part = ray_in[c].at[pl.ds(0, (angles - 1) * hit_rows)]
         return remote(part, part, ray_send.at[c], ray_recv.at[c], (me, strip))
 
-    def pick_copy(c, peer):
+    def pick_copy(c, peer, far):
+        lane = c if far else chunks + c
         return remote(
-            pick_out.at[c, peer], pick_in.at[c, me], pick_send.at[c], pick_recv.at[c],
+            pick_out.at[c, peer], pick_in.at[c, me], pick_send.at[lane], pick_recv.at[lane],
             (peer, strip),
         )
 
-    def pick_all(c):
+    def pick_all(c, far):
+        lane = c if far else chunks + c
+        part = pl.ds(0, len(far_peers) if far else len(near_peers))
         return remote(
-            pick_out.at[c, others], pick_in.at[c, others], pick_send.at[c], pick_recv.at[c],
+            pick_out.at[c, part], pick_in.at[c, part], pick_send.at[lane], pick_recv.at[lane],
             (me, strip),
         )
 
@@ -214,16 +217,6 @@
 
     mine = me // members
     project(lax.rem(mine + groups - 1, groups))
-    loads["dual"].wait()
-    ray_weight = penalty - penalty * penalty * object_step
-    grad_weight = penalty * object_step
-    dual_weight = 1.0 - penalty * object_step
-    for c in range(chunks):
-        part = pl.ds(c, columns, stride=chunks)
-        below = field[part, :] - field_out[c].astype(jnp.float32)
-        wide_out[c][...] = (dual_weight * dual[part, :] + ray_weight * below).astype(
-            wide_out[c].dtype
-        )
     pl.semaphore_wait(barrier, len(ang_peers) + len(strip_peers))
     for peer in strip_peers:
         field_copy(peer).start()
@@ -231,6 +224,16 @@
     if groups > 1:
         project(mine)
     start_rays(0, near_peers)
+    loads["dual"].wait()
+    ray_weight = penalty - penalty * penalty * object_step
+    grad_weight = penalty * object_step
+    dual_weight = 1.0 - penalty * object_step
+    for c in range(chunks):
+        part = pl.ds(c, columns, stride=chunks)
+        below = field[part, :] - field_out[c].astype(jnp.float32)
+        wide_out[c][...] = (dual_weight * dual[part, :] + ray_weight * below).astype(
+            wide_out[c].dtype
+        )
     for c in range(chunks):
         for peer in strip_peers:
             wide_copy(c, peer).start()
@@ -365,9 +368,10 @@
 
     def send_picks(c):
         make_residual(c)
-        for peer in ang_peers:
-            pick_out[c, peer] = rows_half[c][pl.ds(ranges[peer] * RAYS, hit_rows), :]
-            pick_copy(c, peer).start()
+        for far, peers in ((True, far_peers), (False, near_peers)):
+            for peer in peers:
+                pick_out[c, peer] = rows_half[c][pl.ds(ranges[peer] * RAYS, hit_rows), :]
+                pick_copy(c, peer, far).start()
         pick_in[c, me] = rows_half[c][pl.ds(ranges[me] * RAYS, hit_rows), :]
 
     for pair in range(0, frames, 2):
@@ -386,16 +390,27 @@
         send_parts(c)
     for c in range(chunks):
         update(c)
-    for c in range(chunks):
-        pick_all(c).wait_recv()
-        gradient = dot(turned_radon[...], pick_in[c].reshape(angles * hit_rows, slices))
+    def part_gradient(c, group):
+        rows = pick_in[c, pl.ds(group * members, members)].reshape(members * hit_rows, slices)
+        first = pl.multiple_of(group * members * hit_rows, members * hit_rows)
+        return dot(turned_radon[:, pl.ds(first, members * hit_rows)], rows)
+
+    for c in range(chunks):
         part = pl.ds(c, pixels, stride=chunks)
-        volume_next[part, :] = volume[part, :] - volume_step * gradient
+        pick_all(c, False).wait_recv()
+        volume_next[part, :] = volume[part, :] - volume_step * part_gradient(c, mine)
+        if far_peers:
+            pick_all(c, True).wait_recv()
+            volume_next[part, :] = volume_next[part, :] - volume_step * part_gradient(
+                c, 1 - mine
+            )
     for peer in strip_peers:
         field_copy(peer).wait_send()
     for c in range(chunks):
         ray_all(c).wait_send()
-        pick_all(c).wait_send()
+        pick_all(c, False).wait_send()
+        if far_peers:
+            pick_all(c, True).wait_send()
         strip_all(grad_out.at[c], 1 + c).wait_send()
         strip_all(mixed_in.at[c], 1 + 2 * chunks + c).wait_send()
         for peer in strip_peers:
@@ -466,7 +481,8 @@
             pltpu.VMEM((chunks, detector, slices), jnp.float32),
             pltpu.VMEM((pixels, angles * hit_rows), half),
             pltpu.SemaphoreType.DMA((9,)),
-        ] + [pltpu.SemaphoreType.DMA((chunks,))] * 4
+        ] + [pltpu.SemaphoreType.DMA((chunks,))] * 2
+        + [pltpu.SemaphoreType.DMA((2 * chunks,))] * 2
         + [pltpu.SemaphoreType.DMA((1 + 3 * chunks,))] * 2,
         compiler_params=pltpu.CompilerParams(
             collective_id=0, has_side_effects=True, vmem_limit_bytes=VMEM_BYTES

time: 32.5 us -> 32.4 us (level)
  no operation moved by 1% of the time
where the time goes in v8:
time: 32.4 us; the launch traced here: 32.3 us
  Pallas kernels  31.6 us (98%)
  between operations  0.64 us (2%)
    pallas_call x1, Pallas kernels, body(): pl.pallas_call(functools.partial(kernel, angles, strips), out_shape=(pltp...  30.7 us
    pallas_call x1, Pallas kernels, body(): pl.pallas_call(finish, out_shape=[jax.ShapeDtypeStruct(o.shape, o.dtype)...  0.9 us

profile of v8, /device:TPU:0, one launch (start us, length us, event | category | flops | bytes accessed | tf_op | source)
XLA Modules:
  0.0 32.3 jit_solution(7971558147050665932)
XLA Ops:
  0.6 30.7 %shard_map.112 = (f32[512,128]{1,0:T(8,128)S(1)}, f32[512,128]{1,0:T(8,128)S(1)}, f32[512,128]{1,0:T(8,128)S(1)}) custom-call(s32[8]{0:T(128)} %bitcast.15, s32[16]{0:T(128)} %bitcast.16, f32[8,128,128]{2,1,0:T(8,128)} %bitcast.10, f32[2,128,128]{2,1,0:T(8,128)} %probe_hbm.1, f32[512,128]{1,0:T(8,128)} %bitcast.12, f32[512,128]{1,0:T(8,128)} %bitcast.13, ...), custom_call_target="tpu_custom_call" | custom-call | tf_op jit(solution)/shard_map/pallas_call | solution.py:446
  31.4 0.9 %shard_map.113 = (f32[512,128]{1,0:T(8,128)}, f32[512,128]{1,0:T(8,128)}, f32[512,128]{1,0:T(8,128)}) custom-call(f32[512,128]{1,0:T(8,128)S(1)} %get-tuple-element.9.first, f32[512,128]{1,0:T(8,128)S(1)} %get-tuple-element.10.second, f32[512,128]{1,0:T(8,128)S(1)} %get-tuple-element.11.third), custom_call_target="tpu_custom_call" | custom-call | tf_op jit(solution)/shard_map/pallas_call | solution.py:501
